TPU v7x, 1024 devices: a whole 8x8x8 slice. The times are simulated.
1024 devices in a mesh: circ: 32 (over x_hi, z), rad: 16 (over y, x_lo), ax: 2 (over core).
Axes of the slice: x: 8 (x_hi: 4, x_lo: 2; x = x_hi * 2 + x_lo), y: 8, z: 8, core: 2. Of those that a mesh axis runs over, the one named last changes fastest.
Arguments:
- state: float32 [5, 16, 128, 4096], P(None, 'ax', 'rad', 'circ'), may hold values from -6 to 6
- eddy: float32 [16, 128, 4096], P('ax', 'rad', 'circ'), may hold values from 0.02 to 0.2
- offsets: int32 [4], replicated, may hold values from 0 to 31, as said below
- stencil_index: int32 [2, 4, 128, 4], replicated, may hold values from 0 to 127
- stencil_weight: float32 [2, 4, 128, 4], replicated, may hold values from 0.1 to 1
Outputs:
- advanced: float32 [5, 16, 128, 4096], P(None, 'ax', 'rad', 'circ')
Inputs may be any that keep to these rules, and one draw needn't show every extreme that they name: Among the sections' offsets are 16, 31 and 0.
All inputs are finite; a program needn't handle non-finite values.
Results may differ from a plain program's by a relative error of at most 0.00005.
Values sent between devices are 32-bit elements; how exact they have to be, the bound alone decides.
No kernel may reach another device: no remote copies, remote signals or barrier semaphores. Data moves between devices by JAX's collectives and lax.ppermute only.
A program may use at most 32 MiB of HBM per device.

v0:
```python
import jax
import jax.numpy as jnp
from jax import lax
from jax.sharding import PartitionSpec as P

AXIAL_MACH = 0.4
STEP_SIZE = 0.3


def in_order(parts, dim):
    parts = jnp.moveaxis(parts, 0, dim)
    lengths = parts.shape
    return parts.reshape(*lengths[:dim], lengths[dim] * lengths[dim + 1], *lengths[dim + 2 :])


def sent_to_all(x, axis):
    count = lax.axis_size(axis)
    return lax.all_to_all(jnp.broadcast_to(x[None], (count, *x.shape)), axis, 0, 0, tiled=True)


def gathered_copies(x, axis, dim):
    return in_order(sent_to_all(x, axis), dim)


def swapped(value, axis, apart):
    mask = 2**apart
    pairs = [(source, source ^ mask) for source in range(lax.axis_size(axis))]
    return lax.ppermute(value, axis, pairs)


def padded(x, sides, width, wrap):
    for axis, dim in sides:
        count, length = (lax.axis_size(axis), x.shape[dim])
        up = [(i, (i + 1) % count) for i in range(count if wrap else count - 1)]
        down = [(j, i) for i, j in up]
        last = lax.slice_in_dim(x, length - width, length, axis=dim)
        leading = lax.slice_in_dim(x, 0, width, axis=dim)
        before = lax.ppermute(last, axis, up)
        after = lax.ppermute(leading, axis, down)
        x = jnp.concatenate([before, x, after], axis=dim)
    return x


def interp_matrix(index_rows, weight_rows):
    width = index_rows.shape[0]
    onehot = (index_rows[:, :, None] == jnp.arange(width, dtype=jnp.int32)[None, None, :]).astype(
        jnp.float32
    )
    normed = weight_rows / jnp.sum(weight_rows, axis=1, keepdims=True)
    return jnp.sum(normed[:, :, None] * onehot, axis=1)


def tendency(
    center, circ_low, circ_high, radial_low, radial_high, axial_low, axial_high, swirl, eddy
):
    diff_circ = 0.5 * (circ_high - circ_low)
    diff_radial = 0.5 * (radial_high - radial_low)
    diff_axial = 0.5 * (axial_high - axial_low)
    laplace = (
        circ_high + circ_low + (radial_high + radial_low) + (axial_high + axial_low) - 6.0 * center
    )
    advect = swirl * diff_circ + AXIAL_MACH * diff_axial
    diverge = diff_circ[1] + diff_radial[2] + diff_axial[3]
    flux = jnp.stack([diverge, diff_circ[4], diff_radial[4], diff_axial[4], diverge])
    return -advect - flux + eddy[None] * laplace


def facing_ghost(field, offset_now, index_section, weight_section):
    sectors = lax.axis_size("circ")
    cycle_index = lax.axis_index("circ")
    is_rotor = lax.axis_index("ax") == 1
    plane_out = jnp.where(is_rotor, field[:, 0], field[:, -1])
    amount = jnp.where(is_rotor, offset_now, (sectors - offset_now) % sectors)
    planes = gathered_copies(plane_out[None], "circ", 0)
    source = (cycle_index + sectors - amount) % sectors
    carried = lax.dynamic_index_in_dim(planes, source, 0, keepdims=False)
    received = swapped(carried, "ax", 0)
    table_side = lax.axis_index("ax")
    matrix = interp_matrix(index_section[table_side], weight_section[table_side])
    width = received.shape[-1]
    flat_rows = received.reshape(-1, width)
    ghost = jnp.dot(
        flat_rows, matrix.T, precision=lax.Precision.HIGHEST, preferred_element_type=jnp.float32
    )
    return ghost.reshape(received.shape)


def section_tendency(field, eddy, offset_now, index_section, weight_section):
    is_rotor = lax.axis_index("ax") == 1
    circ_padded = padded(field, (("circ", 3),), 1, True)
    radial_padded = padded(field, (("rad", 2),), 1, False)
    ghost = facing_ghost(field, offset_now, index_section, weight_section)
    zero_plane = jnp.zeros_like(ghost)
    below = jnp.where(is_rotor, ghost, zero_plane)[:, None]
    above = jnp.where(is_rotor, zero_plane, ghost)[:, None]
    axial_low = jnp.concatenate([below, field[:, :-1]], axis=1)
    axial_high = jnp.concatenate([field[:, 1:], above], axis=1)
    swirl = jnp.where(is_rotor, -0.3, 0.2).astype(jnp.float32)
    return tendency(
        field,
        circ_padded[..., :-2],
        circ_padded[..., 2:],
        radial_padded[:, :, :-2],
        radial_padded[:, :, 2:],
        axial_low,
        axial_high,
        swirl,
        eddy,
    )


def local(state, eddy, offsets, stencil_index, stencil_weight):

    def slope(field, section):
        return section_tendency(
            field, eddy, offsets[section], stencil_index[:, section], stencil_weight[:, section]
        )

    slope_one = slope(state, 0)
    slope_two = slope(state + 0.5 * STEP_SIZE * slope_one, 1)
    slope_three = slope(state + 0.5 * STEP_SIZE * slope_two, 2)
    slope_four = slope(state + STEP_SIZE * slope_three, 3)
    return state + STEP_SIZE / 6.0 * (slope_one + 2.0 * slope_two + 2.0 * slope_three + slope_four)


def solution(mesh):
    return jax.shard_map(
        local,
        mesh=mesh,
        in_specs=(P(None, "ax", "rad", "circ"), P("ax", "rad", "circ"), P(), P(), P()),
        out_specs=P(None, "ax", "rad", "circ"),
        check_vma=False,
    )
```

profile of v0, /device:TPU:48, one launch (start us, length us, event | category | flops | bytes accessed | tf_op | source)
XLA Modules:
  0.0 165.0 jit_solution(6772031603113200903)
XLA Ops:
  0.0 1.0 fusion.38
  1.0 3.2 %collective-permute-start.3 = (f32[5,8,1,128]{3,2,1,0:T(1,128)S(1)}, f32[5,8,1,128]{3,2,1,0:T(1,128)S(1)}, u32[]{:S(2)}, u32[]{:S(2)}) collective-permute-start(f32[5,8,1,128]{3,2,1,0:T(1,128)S(1)} %get-tuple-element.40), channel_id=1, source_target_pairs={{2,0},{4,2},{6,4},{8,6},{10,8},{12,10},{14,12},{16,14},{18,16},{20... | collective-permute-start | bytes 61448 | tf_op jit(solution)/shard_map/ppermute | solution.py:39
  4.2 2.7 %collective-permute-start.4 = (f32[5,8,1,128]{3,2,1,0:T(1,128)S(1)}, f32[5,8,1,128]{3,2,1,0:T(1,128)S(1)}, u32[]{:S(2)}, u32[]{:S(2)}) collective-permute-start(f32[5,8,1,128]{3,2,1,0:T(1,128)S(1)} %get-tuple-element.39), channel_id=1, source_target_pairs={{0,2},{2,4},{4,6},{6,8},{8,10},{10,12},{12,14},{14,16},{16,18},{18... | collective-permute-start | bytes 61448 | tf_op jit(solution)/shard_map/ppermute | solution.py:38
  6.9 0.8 select_bitcast_fusion.8
  7.6 0.9 broadcast_in_dim.24
  8.5 22.1 %all-to-all-start = ((f32[32,1,5,8,128]{4,3,2,1,0:T(8,128)}), f32[32,1,5,8,128]{4,3,2,1,0:T(8,128)S(1)}, u32[]{:S(2)}, u32[]{:S(2)}) async-start(f32[32,1,5,8,128]{4,3,2,1,0:T(8,128)} %broadcast_in_dim.24), calls=%async_computation | async-start | bytes 1310720 | tf_op jit(solution)/shard_map/all_to_all | solution.py:18
  30.7 0.1 fusion.36
  30.8 0.0 copy-start.4
  30.8 8.0 %collective-permute-start = (f32[5,8,8,1]{3,2,1,0:T(8,128)S(1)}, f32[5,8,8,1]{3,2,1,0:T(8,128)S(1)}, u32[]{:S(2)}, u32[]{:S(2)}) collective-permute-start(f32[5,8,8,1]{3,2,1,0:T(8,128)S(1)} %get-tuple-element.36), channel_id=1, source_target_pairs={{32,0},{64,32},{96,64},{128,96},{160,128},{192,160},{224,192},{256... | collective-permute-start | bytes 3848 | tf_op jit(solution)/shard_map/ppermute | solution.py:39
  38.8 1.9 %collective-permute-start.1 = (f32[5,8,8,1]{3,2,1,0:T(8,128)S(1)}, f32[5,8,8,1]{3,2,1,0:T(8,128)S(1)}, u32[]{:S(2)}, u32[]{:S(2)}) collective-permute-start(f32[5,8,8,1]{3,2,1,0:T(8,128)S(1)} %get-tuple-element.35), channel_id=1, source_target_pairs={{0,32},{32,64},{64,96},{96,128},{128,160},{160,192},{192,224},{224... | collective-permute-start | bytes 3848 | tf_op jit(solution)/shard_map/ppermute | solution.py:38
  40.7 0.7 fusion.41
  42.8 0.7 copy-done.2
  43.6 0.7 copy-done.3
  44.3 0.2 select_reduce_fusion.3
  44.5 6.2 %all-to-all-done = f32[32,1,5,8,128]{4,3,2,1,0:T(8,128)S(1)} async-done(((f32[32,1,5,8,128]{4,3,2,1,0:T(8,128)}), f32[32,1,5,8,128]{4,3,2,1,0:T(8,128)S(1)}, u32[]{:S(2)}, u32[]{:S(2)}) %all-to-all-start) | async-done | bytes 655392 | tf_op jit(solution)/shard_map/all_to_all | solution.py:18
  50.7 1.9 %collective-permute-start.2 = (f32[5,8,128]{2,1,0:T(8,128)S(1)}, f32[5,8,128]{2,1,0:T(8,128)S(1)}, u32[]{:S(2)}, u32[]{:S(2)}) collective-permute-start(f32[5,8,128]{2,1,0:T(8,128)S(1)} %dynamic-slice_bitcast_fusion.3), channel_id=1, source_target_pairs={{0,1},{1,0},{2,3},{3,2},{4,5},{5,4},{6,7},{7,6},{8,9},{9,8},{10,11... | collective-permute-start | bytes 61448 | tf_op jit(solution)/shard_map/ppermute | solution.py:28
  52.6 1.2 collective-permute-done
  53.8 0.2 collective-permute-done.1
  54.0 0.2 subtract_multiply_fusion.4
  54.2 0.2 select_bitcast_fusion.7
  54.6 0.7 copy-done.1
  55.3 0.2 multiply_add_fusion.5
  55.6 0.9 broadcast_in_dim.27
  56.4 10.6 %all-to-all-start.1 = ((f32[32,1,5,8,128]{4,3,2,1,0:T(8,128)}), f32[32,1,5,8,128]{4,3,2,1,0:T(8,128)S(1)}, u32[]{:S(2)}, u32[]{:S(2)}) async-start(f32[32,1,5,8,128]{4,3,2,1,0:T(8,128)} %broadcast_in_dim.27), calls=%async_computation.1 | async-start | bytes 1310720 | tf_op jit(solution)/shard_map/all_to_all | solution.py:18
  68.2 0.2 select_reduce_fusion.2
  68.5 2.7 %collective-permute-start.9 = (f32[5,8,1,128]{3,2,1,0:T(1,128)S(1)}, f32[5,8,1,128]{3,2,1,0:T(1,128)S(1)}, u32[]{:S(2)}, u32[]{:S(2)}) collective-permute-start(f32[5,8,1,128]{3,2,1,0:T(1,128)S(1)} %get-tuple-element.32), channel_id=1, source_target_pairs={{0,2},{2,4},{4,6},{6,8},{8,10},{10,12},{12,14},{14,16},{16,18},{18... | collective-permute-start | bytes 61448 | tf_op jit(solution)/shard_map/ppermute | solution.py:38
  71.2 4.1 %collective-permute-start.8 = (f32[5,8,1,128]{3,2,1,0:T(1,128)S(1)}, f32[5,8,1,128]{3,2,1,0:T(1,128)S(1)}, u32[]{:S(2)}, u32[]{:S(2)}) collective-permute-start(f32[5,8,1,128]{3,2,1,0:T(1,128)S(1)} %get-tuple-element.31), channel_id=1, source_target_pairs={{2,0},{4,2},{6,4},{8,6},{10,8},{12,10},{14,12},{16,14},{18,16},{20... | collective-permute-start | bytes 61448 | tf_op jit(solution)/shard_map/ppermute | solution.py:39
  75.2 0.1 fusion.33
  75.4 8.0 %collective-permute-start.5 = (f32[5,8,8,1]{3,2,1,0:T(8,128)S(1)}, f32[5,8,8,1]{3,2,1,0:T(8,128)S(1)}, u32[]{:S(2)}, u32[]{:S(2)}) collective-permute-start(f32[5,8,8,1]{3,2,1,0:T(8,128)S(1)} %get-tuple-element.28), channel_id=1, source_target_pairs={{32,0},{64,32},{96,64},{128,96},{160,128},{192,160},{224,192},{256... | collective-permute-start | bytes 3848 | tf_op jit(solution)/shard_map/ppermute | solution.py:39
  83.4 1.9 %collective-permute-start.6 = (f32[5,8,8,1]{3,2,1,0:T(8,128)S(1)}, f32[5,8,8,1]{3,2,1,0:T(8,128)S(1)}, u32[]{:S(2)}, u32[]{:S(2)}) collective-permute-start(f32[5,8,8,1]{3,2,1,0:T(8,128)S(1)} %get-tuple-element.27), channel_id=1, source_target_pairs={{0,32},{32,64},{64,96},{96,128},{128,160},{160,192},{192,224},{224... | collective-permute-start | bytes 3848 | tf_op jit(solution)/shard_map/ppermute | solution.py:38
  85.3 4.3 %all-to-all-done.1 = f32[32,1,5,8,128]{4,3,2,1,0:T(8,128)S(1)} async-done(((f32[32,1,5,8,128]{4,3,2,1,0:T(8,128)}), f32[32,1,5,8,128]{4,3,2,1,0:T(8,128)S(1)}, u32[]{:S(2)}, u32[]{:S(2)}) %all-to-all-start.1) | async-done | bytes 655392 | tf_op jit(solution)/shard_map/all_to_all | solution.py:18
  89.6 1.9 %collective-permute-start.7 = (f32[5,8,128]{2,1,0:T(8,128)S(1)}, f32[5,8,128]{2,1,0:T(8,128)S(1)}, u32[]{:S(2)}, u32[]{:S(2)}) collective-permute-start(f32[5,8,128]{2,1,0:T(8,128)S(1)} %dynamic-slice_bitcast_fusion.2), channel_id=1, source_target_pairs={{0,1},{1,0},{2,3},{3,2},{4,5},{5,4},{6,7},{7,6},{8,9},{9,8},{10,11... | collective-permute-start | bytes 61448 | tf_op jit(solution)/shard_map/ppermute | solution.py:28
  91.5 5.3 %collective-permute-done.6 = f32[5,8,8,1]{3,2,1,0:T(8,128)S(1)} collective-permute-done((f32[5,8,8,1]{3,2,1,0:T(8,128)S(1)}, f32[5,8,8,1]{3,2,1,0:T(8,128)S(1)}, u32[]{:S(2)}, u32[]{:S(2)}) %collective-permute-start.6) | collective-permute-done | bytes 1312 | tf_op jit(solution)/shard_map/ppermute | solution.py:38
  96.8 0.2 broadcast_multiply_fusion.2
  97.0 0.2 select_bitcast_fusion.5
  97.4 0.2 multiply_add_fusion.3
  97.6 0.9 broadcast_in_dim.30
  98.5 3.9 %all-to-all-start.2 = ((f32[32,1,5,8,128]{4,3,2,1,0:T(8,128)}), f32[32,1,5,8,128]{4,3,2,1,0:T(8,128)S(1)}, u32[]{:S(2)}, u32[]{:S(2)}) async-start(f32[32,1,5,8,128]{4,3,2,1,0:T(8,128)} %broadcast_in_dim.30), calls=%async_computation.2 | async-start | bytes 1310720 | tf_op jit(solution)/shard_map/all_to_all | solution.py:18
  103.8 0.2 select_reduce_fusion.1
  104.0 1.9 %collective-permute-start.14 = (f32[5,8,1,128]{3,2,1,0:T(1,128)S(1)}, f32[5,8,1,128]{3,2,1,0:T(1,128)S(1)}, u32[]{:S(2)}, u32[]{:S(2)}) collective-permute-start(f32[5,8,1,128]{3,2,1,0:T(1,128)S(1)} %get-tuple-element.24), channel_id=1, source_target_pairs={{0,2},{2,4},{4,6},{6,8},{8,10},{10,12},{12,14},{14,16},{16,18},{18... | collective-permute-start | bytes 61448 | tf_op jit(solution)/shard_map/ppermute | solution.py:38
  105.9 4.8 %collective-permute-start.13 = (f32[5,8,1,128]{3,2,1,0:T(1,128)S(1)}, f32[5,8,1,128]{3,2,1,0:T(1,128)S(1)}, u32[]{:S(2)}, u32[]{:S(2)}) collective-permute-start(f32[5,8,1,128]{3,2,1,0:T(1,128)S(1)} %get-tuple-element.23), channel_id=1, source_target_pairs={{2,0},{4,2},{6,4},{8,6},{10,8},{12,10},{14,12},{16,14},{18,16},{20... | collective-permute-start | bytes 61448 | tf_op jit(solution)/shard_map/ppermute | solution.py:39
  110.8 0.1 fusion.30
  110.9 8.0 %collective-permute-start.10 = (f32[5,8,8,1]{3,2,1,0:T(8,128)S(1)}, f32[5,8,8,1]{3,2,1,0:T(8,128)S(1)}, u32[]{:S(2)}, u32[]{:S(2)}) collective-permute-start(f32[5,8,8,1]{3,2,1,0:T(8,128)S(1)} %get-tuple-element.20), channel_id=1, source_target_pairs={{32,0},{64,32},{96,64},{128,96},{160,128},{192,160},{224,192},{256... | collective-permute-start | bytes 3848 | tf_op jit(solution)/shard_map/ppermute | solution.py:39
  118.9 1.9 %collective-permute-start.11 = (f32[5,8,8,1]{3,2,1,0:T(8,128)S(1)}, f32[5,8,8,1]{3,2,1,0:T(8,128)S(1)}, u32[]{:S(2)}, u32[]{:S(2)}) collective-permute-start(f32[5,8,8,1]{3,2,1,0:T(8,128)S(1)} %get-tuple-element.19), channel_id=1, source_target_pairs={{0,32},{32,64},{64,96},{96,128},{128,160},{160,192},{192,224},{224... | collective-permute-start | bytes 3848 | tf_op jit(solution)/shard_map/ppermute | solution.py:38
  120.8 4.5 %all-to-all-done.2 = f32[32,1,5,8,128]{4,3,2,1,0:T(8,128)S(1)} async-done(((f32[32,1,5,8,128]{4,3,2,1,0:T(8,128)}), f32[32,1,5,8,128]{4,3,2,1,0:T(8,128)S(1)}, u32[]{:S(2)}, u32[]{:S(2)}) %all-to-all-start.2) | async-done | bytes 655392 | tf_op jit(solution)/shard_map/all_to_all | solution.py:18
  125.4 1.9 %collective-permute-start.12 = (f32[5,8,128]{2,1,0:T(8,128)S(1)}, f32[5,8,128]{2,1,0:T(8,128)S(1)}, u32[]{:S(2)}, u32[]{:S(2)}) collective-permute-start(f32[5,8,128]{2,1,0:T(8,128)S(1)} %dynamic-slice_bitcast_fusion.1), channel_id=1, source_target_pairs={{0,1},{1,0},{2,3},{3,2},{4,5},{5,4},{6,7},{7,6},{8,9},{9,8},{10,11... | collective-permute-start | bytes 61448 | tf_op jit(solution)/shard_map/ppermute | solution.py:28
  127.3 3.1 %collective-permute-done.11 = f32[5,8,8,1]{3,2,1,0:T(8,128)S(1)} collective-permute-done((f32[5,8,8,1]{3,2,1,0:T(8,128)S(1)}, f32[5,8,8,1]{3,2,1,0:T(8,128)S(1)}, u32[]{:S(2)}, u32[]{:S(2)}) %collective-permute-start.11) | collective-permute-done | bytes 1312 | tf_op jit(solution)/shard_map/ppermute | solution.py:38
  130.4 0.2 broadcast_multiply_fusion.1
  130.7 0.2 select_bitcast_fusion.3
  131.0 0.2 multiply_add_fusion.1
  131.3 0.9 broadcast_in_dim.33
  132.1 4.9 %all-to-all-start.3 = ((f32[32,1,5,8,128]{4,3,2,1,0:T(8,128)}), f32[32,1,5,8,128]{4,3,2,1,0:T(8,128)S(1)}, u32[]{:S(2)}, u32[]{:S(2)}) async-start(f32[32,1,5,8,128]{4,3,2,1,0:T(8,128)} %broadcast_in_dim.33), calls=%async_computation.3 | async-start | bytes 1310720 | tf_op jit(solution)/shard_map/all_to_all | solution.py:18
  138.4 0.2 select_reduce_fusion
  138.6 0.1 fusion.27
  138.8 8.0 %collective-permute-start.15 = (f32[5,8,8,1]{3,2,1,0:T(8,128)S(1)}, f32[5,8,8,1]{3,2,1,0:T(8,128)S(1)}, u32[]{:S(2)}, u32[]{:S(2)}) collective-permute-start(f32[5,8,8,1]{3,2,1,0:T(8,128)S(1)} %get-tuple-element.12), channel_id=1, source_target_pairs={{32,0},{64,32},{96,64},{128,96},{160,128},{192,160},{224,192},{256... | collective-permute-start | bytes 3848 | tf_op jit(solution)/shard_map/ppermute | solution.py:39
  146.8 1.9 %collective-permute-start.16 = (f32[5,8,8,1]{3,2,1,0:T(8,128)S(1)}, f32[5,8,8,1]{3,2,1,0:T(8,128)S(1)}, u32[]{:S(2)}, u32[]{:S(2)}) collective-permute-start(f32[5,8,8,1]{3,2,1,0:T(8,128)S(1)} %get-tuple-element.11), channel_id=1, source_target_pairs={{0,32},{32,64},{64,96},{96,128},{128,160},{160,192},{192,224},{224... | collective-permute-start | bytes 3848 | tf_op jit(solution)/shard_map/ppermute | solution.py:38
  148.7 4.1 %collective-permute-start.19 = (f32[5,8,1,128]{3,2,1,0:T(1,128)S(1)}, f32[5,8,1,128]{3,2,1,0:T(1,128)S(1)}, u32[]{:S(2)}, u32[]{:S(2)}) collective-permute-start(f32[5,8,1,128]{3,2,1,0:T(1,128)S(1)} %get-tuple-element.13), channel_id=1, source_target_pairs={{0,2},{2,4},{4,6},{6,8},{8,10},{10,12},{12,14},{14,16},{16,18},{18... | collective-permute-start | bytes 61448 | tf_op jit(solution)/shard_map/ppermute | solution.py:38
  152.8 2.6 %collective-permute-start.18 = (f32[5,8,1,128]{3,2,1,0:T(1,128)S(1)}, f32[5,8,1,128]{3,2,1,0:T(1,128)S(1)}, u32[]{:S(2)}, u32[]{:S(2)}) collective-permute-start(f32[5,8,1,128]{3,2,1,0:T(1,128)S(1)} %get-tuple-element.14), channel_id=1, source_target_pairs={{2,0},{4,2},{6,4},{8,6},{10,8},{12,10},{14,12},{16,14},{18,16},{20... | collective-permute-start | bytes 61448 | tf_op jit(solution)/shard_map/ppermute | solution.py:39
  155.5 2.8 %all-to-all-done.3 = f32[32,1,5,8,128]{4,3,2,1,0:T(8,128)S(1)} async-done(((f32[32,1,5,8,128]{4,3,2,1,0:T(8,128)}), f32[32,1,5,8,128]{4,3,2,1,0:T(8,128)S(1)}, u32[]{:S(2)}, u32[]{:S(2)}) %all-to-all-start.3) | async-done | bytes 655392 | tf_op jit(solution)/shard_map/all_to_all | solution.py:18
  158.3 1.9 %collective-permute-start.17 = (f32[5,8,128]{2,1,0:T(8,128)S(1)}, f32[5,8,128]{2,1,0:T(8,128)S(1)}, u32[]{:S(2)}, u32[]{:S(2)}) collective-permute-start(f32[5,8,128]{2,1,0:T(8,128)S(1)} %dynamic-slice_bitcast_fusion), channel_id=1, source_target_pairs={{0,1},{1,0},{2,3},{3,2},{4,5},{5,4},{6,7},{7,6},{8,9},{9,8},{10,11... | collective-permute-start | bytes 61448 | tf_op jit(solution)/shard_map/ppermute | solution.py:28
  160.2 3.1 %collective-permute-done.16 = f32[5,8,8,1]{3,2,1,0:T(8,128)S(1)} collective-permute-done((f32[5,8,8,1]{3,2,1,0:T(8,128)S(1)}, f32[5,8,8,1]{3,2,1,0:T(8,128)S(1)}, u32[]{:S(2)}, u32[]{:S(2)}) %collective-permute-start.16) | collective-permute-done | bytes 1312 | tf_op jit(solution)/shard_map/ppermute | solution.py:38
  163.3 0.2 broadcast_multiply_fusion
  163.5 0.2 select_bitcast_fusion.1
  163.9 1.1 multiply_add_fusion
  (73 shorter events, 0.7 us)
Async XLA Ops:
  1.0 53.0 %collective-permute-start.3 = (f32[5,8,1,128]{3,2,1,0:T(1,128)S(1)}, f32[5,8,1,128]{3,2,1,0:T(1,128)S(1)}, u32[]{:S(2)}, u32[]{:S(2)}) collective-permute-start(f32[5,8,1,128]{3,2,1,0:T(1,128)S(1)} %get-tuple-element.40), channel_id=1, source_target_pairs={{2,0},{4,2},{6,4},{8,6},{10,8},{12,10},{14,12},{16,14},{18,16},{20... | collective-permute-start | bytes 61448 | tf_op jit(solution)/shard_map/ppermute | solution.py:39
  4.2 49.8 %collective-permute-start.4 = (f32[5,8,1,128]{3,2,1,0:T(1,128)S(1)}, f32[5,8,1,128]{3,2,1,0:T(1,128)S(1)}, u32[]{:S(2)}, u32[]{:S(2)}) collective-permute-start(f32[5,8,1,128]{3,2,1,0:T(1,128)S(1)} %get-tuple-element.39), channel_id=1, source_target_pairs={{0,2},{2,4},{4,6},{6,8},{8,10},{10,12},{12,14},{14,16},{16,18},{18... | collective-permute-start | bytes 61448 | tf_op jit(solution)/shard_map/ppermute | solution.py:38
  8.5 22.1 %copy-start = (f32[5,8,8,128]{3,2,1,0:T(8,128)S(1)}, f32[5,8,8,128]{3,2,1,0:T(8,128)}, u32[]{:S(2)}) copy-start(f32[5,8,8,128]{3,2,1,0:T(8,128)} %param.5) | copy-start | bytes 491524
  8.5 42.1 %all-to-all-start = ((f32[32,1,5,8,128]{4,3,2,1,0:T(8,128)}), f32[32,1,5,8,128]{4,3,2,1,0:T(8,128)S(1)}, u32[]{:S(2)}, u32[]{:S(2)}) async-start(f32[32,1,5,8,128]{4,3,2,1,0:T(8,128)} %broadcast_in_dim.24), calls=%async_computation | async-start | bytes 1310720 | tf_op jit(solution)/shard_map/all_to_all | solution.py:18
  30.8 10.0 %copy-start.4 = (s32[4]{0:T(128)S(1)}, s32[4]{0:T(128)}, u32[]{:S(2)}) copy-start(s32[4]{0:T(128)} %param.7) | copy-start | bytes 52
  30.8 23.0 %collective-permute-start = (f32[5,8,8,1]{3,2,1,0:T(8,128)S(1)}, f32[5,8,8,1]{3,2,1,0:T(8,128)S(1)}, u32[]{:S(2)}, u32[]{:S(2)}) collective-permute-start(f32[5,8,8,1]{3,2,1,0:T(8,128)S(1)} %get-tuple-element.36), channel_id=1, source_target_pairs={{32,0},{64,32},{96,64},{128,96},{160,128},{192,160},{224,192},{256... | collective-permute-start | bytes 3848 | tf_op jit(solution)/shard_map/ppermute | solution.py:39
  38.8 15.2 %collective-permute-start.1 = (f32[5,8,8,1]{3,2,1,0:T(8,128)S(1)}, f32[5,8,8,1]{3,2,1,0:T(8,128)S(1)}, u32[]{:S(2)}, u32[]{:S(2)}) collective-permute-start(f32[5,8,8,1]{3,2,1,0:T(8,128)S(1)} %get-tuple-element.35), channel_id=1, source_target_pairs={{0,32},{32,64},{64,96},{96,128},{128,160},{160,192},{192,224},{224... | collective-permute-start | bytes 3848 | tf_op jit(solution)/shard_map/ppermute | solution.py:38
  42.8 0.7 copy-start.2
  43.5 0.7 copy-start.3
  50.7 3.5 %collective-permute-start.2 = (f32[5,8,128]{2,1,0:T(8,128)S(1)}, f32[5,8,128]{2,1,0:T(8,128)S(1)}, u32[]{:S(2)}, u32[]{:S(2)}) collective-permute-start(f32[5,8,128]{2,1,0:T(8,128)S(1)} %dynamic-slice_bitcast_fusion.3), channel_id=1, source_target_pairs={{0,1},{1,0},{2,3},{3,2},{4,5},{5,4},{6,7},{7,6},{8,9},{9,8},{10,11... | collective-permute-start | bytes 61448 | tf_op jit(solution)/shard_map/ppermute | solution.py:28
  54.5 0.8 copy-start.1
  56.4 33.1 %all-to-all-start.1 = ((f32[32,1,5,8,128]{4,3,2,1,0:T(8,128)}), f32[32,1,5,8,128]{4,3,2,1,0:T(8,128)S(1)}, u32[]{:S(2)}, u32[]{:S(2)}) async-start(f32[32,1,5,8,128]{4,3,2,1,0:T(8,128)} %broadcast_in_dim.27), calls=%async_computation.1 | async-start | bytes 1310720 | tf_op jit(solution)/shard_map/all_to_all | solution.py:18
  68.5 28.3 %collective-permute-start.9 = (f32[5,8,1,128]{3,2,1,0:T(1,128)S(1)}, f32[5,8,1,128]{3,2,1,0:T(1,128)S(1)}, u32[]{:S(2)}, u32[]{:S(2)}) collective-permute-start(f32[5,8,1,128]{3,2,1,0:T(1,128)S(1)} %get-tuple-element.32), channel_id=1, source_target_pairs={{0,2},{2,4},{4,6},{6,8},{8,10},{10,12},{12,14},{14,16},{16,18},{18... | collective-permute-start | bytes 61448 | tf_op jit(solution)/shard_map/ppermute | solution.py:38
  71.2 25.6 %collective-permute-start.8 = (f32[5,8,1,128]{3,2,1,0:T(1,128)S(1)}, f32[5,8,1,128]{3,2,1,0:T(1,128)S(1)}, u32[]{:S(2)}, u32[]{:S(2)}) collective-permute-start(f32[5,8,1,128]{3,2,1,0:T(1,128)S(1)} %get-tuple-element.31), channel_id=1, source_target_pairs={{2,0},{4,2},{6,4},{8,6},{10,8},{12,10},{14,12},{16,14},{18,16},{20... | collective-permute-start | bytes 61448 | tf_op jit(solution)/shard_map/ppermute | solution.py:39
  75.4 16.2 %collective-permute-start.5 = (f32[5,8,8,1]{3,2,1,0:T(8,128)S(1)}, f32[5,8,8,1]{3,2,1,0:T(8,128)S(1)}, u32[]{:S(2)}, u32[]{:S(2)}) collective-permute-start(f32[5,8,8,1]{3,2,1,0:T(8,128)S(1)} %get-tuple-element.28), channel_id=1, source_target_pairs={{32,0},{64,32},{96,64},{128,96},{160,128},{192,160},{224,192},{256... | collective-permute-start | bytes 3848 | tf_op jit(solution)/shard_map/ppermute | solution.py:39
  83.4 13.4 %collective-permute-start.6 = (f32[5,8,8,1]{3,2,1,0:T(8,128)S(1)}, f32[5,8,8,1]{3,2,1,0:T(8,128)S(1)}, u32[]{:S(2)}, u32[]{:S(2)}) collective-permute-start(f32[5,8,8,1]{3,2,1,0:T(8,128)S(1)} %get-tuple-element.27), channel_id=1, source_target_pairs={{0,32},{32,64},{64,96},{96,128},{128,160},{160,192},{192,224},{224... | collective-permute-start | bytes 3848 | tf_op jit(solution)/shard_map/ppermute | solution.py:38
  89.6 7.4 %collective-permute-start.7 = (f32[5,8,128]{2,1,0:T(8,128)S(1)}, f32[5,8,128]{2,1,0:T(8,128)S(1)}, u32[]{:S(2)}, u32[]{:S(2)}) collective-permute-start(f32[5,8,128]{2,1,0:T(8,128)S(1)} %dynamic-slice_bitcast_fusion.2), channel_id=1, source_target_pairs={{0,1},{1,0},{2,3},{3,2},{4,5},{5,4},{6,7},{7,6},{8,9},{9,8},{10,11... | collective-permute-start | bytes 61448 | tf_op jit(solution)/shard_map/ppermute | solution.py:28
  98.5 26.9 %all-to-all-start.2 = ((f32[32,1,5,8,128]{4,3,2,1,0:T(8,128)}), f32[32,1,5,8,128]{4,3,2,1,0:T(8,128)S(1)}, u32[]{:S(2)}, u32[]{:S(2)}) async-start(f32[32,1,5,8,128]{4,3,2,1,0:T(8,128)} %broadcast_in_dim.30), calls=%async_computation.2 | async-start | bytes 1310720 | tf_op jit(solution)/shard_map/all_to_all | solution.py:18
  104.0 26.4 %collective-permute-start.14 = (f32[5,8,1,128]{3,2,1,0:T(1,128)S(1)}, f32[5,8,1,128]{3,2,1,0:T(1,128)S(1)}, u32[]{:S(2)}, u32[]{:S(2)}) collective-permute-start(f32[5,8,1,128]{3,2,1,0:T(1,128)S(1)} %get-tuple-element.24), channel_id=1, source_target_pairs={{0,2},{2,4},{4,6},{6,8},{8,10},{10,12},{12,14},{14,16},{16,18},{18... | collective-permute-start | bytes 61448 | tf_op jit(solution)/shard_map/ppermute | solution.py:38
  105.9 24.5 %collective-permute-start.13 = (f32[5,8,1,128]{3,2,1,0:T(1,128)S(1)}, f32[5,8,1,128]{3,2,1,0:T(1,128)S(1)}, u32[]{:S(2)}, u32[]{:S(2)}) collective-permute-start(f32[5,8,1,128]{3,2,1,0:T(1,128)S(1)} %get-tuple-element.23), channel_id=1, source_target_pairs={{2,0},{4,2},{6,4},{8,6},{10,8},{12,10},{14,12},{16,14},{18,16},{20... | collective-permute-start | bytes 61448 | tf_op jit(solution)/shard_map/ppermute | solution.py:39
  110.9 16.4 %collective-permute-start.10 = (f32[5,8,8,1]{3,2,1,0:T(8,128)S(1)}, f32[5,8,8,1]{3,2,1,0:T(8,128)S(1)}, u32[]{:S(2)}, u32[]{:S(2)}) collective-permute-start(f32[5,8,8,1]{3,2,1,0:T(8,128)S(1)} %get-tuple-element.20), channel_id=1, source_target_pairs={{32,0},{64,32},{96,64},{128,96},{160,128},{192,160},{224,192},{256... | collective-permute-start | bytes 3848 | tf_op jit(solution)/shard_map/ppermute | solution.py:39
  118.9 11.5 %collective-permute-start.11 = (f32[5,8,8,1]{3,2,1,0:T(8,128)S(1)}, f32[5,8,8,1]{3,2,1,0:T(8,128)S(1)}, u32[]{:S(2)}, u32[]{:S(2)}) collective-permute-start(f32[5,8,8,1]{3,2,1,0:T(8,128)S(1)} %get-tuple-element.19), channel_id=1, source_target_pairs={{0,32},{32,64},{64,96},{96,128},{128,160},{160,192},{192,224},{224... | collective-permute-start | bytes 3848 | tf_op jit(solution)/shard_map/ppermute | solution.py:38
  125.4 5.3 %collective-permute-start.12 = (f32[5,8,128]{2,1,0:T(8,128)S(1)}, f32[5,8,128]{2,1,0:T(8,128)S(1)}, u32[]{:S(2)}, u32[]{:S(2)}) collective-permute-start(f32[5,8,128]{2,1,0:T(8,128)S(1)} %dynamic-slice_bitcast_fusion.1), channel_id=1, source_target_pairs={{0,1},{1,0},{2,3},{3,2},{4,5},{5,4},{6,7},{7,6},{8,9},{9,8},{10,11... | collective-permute-start | bytes 61448 | tf_op jit(solution)/shard_map/ppermute | solution.py:28
  132.1 26.2 %all-to-all-start.3 = ((f32[32,1,5,8,128]{4,3,2,1,0:T(8,128)}), f32[32,1,5,8,128]{4,3,2,1,0:T(8,128)S(1)}, u32[]{:S(2)}, u32[]{:S(2)}) async-start(f32[32,1,5,8,128]{4,3,2,1,0:T(8,128)} %broadcast_in_dim.33), calls=%async_computation.3 | async-start | bytes 1310720 | tf_op jit(solution)/shard_map/all_to_all | solution.py:18
  138.8 21.5 %collective-permute-start.15 = (f32[5,8,8,1]{3,2,1,0:T(8,128)S(1)}, f32[5,8,8,1]{3,2,1,0:T(8,128)S(1)}, u32[]{:S(2)}, u32[]{:S(2)}) collective-permute-start(f32[5,8,8,1]{3,2,1,0:T(8,128)S(1)} %get-tuple-element.12), channel_id=1, source_target_pairs={{32,0},{64,32},{96,64},{128,96},{160,128},{192,160},{224,192},{256... | collective-permute-start | bytes 3848 | tf_op jit(solution)/shard_map/ppermute | solution.py:39
  146.8 16.5 %collective-permute-start.16 = (f32[5,8,8,1]{3,2,1,0:T(8,128)S(1)}, f32[5,8,8,1]{3,2,1,0:T(8,128)S(1)}, u32[]{:S(2)}, u32[]{:S(2)}) collective-permute-start(f32[5,8,8,1]{3,2,1,0:T(8,128)S(1)} %get-tuple-element.11), channel_id=1, source_target_pairs={{0,32},{32,64},{64,96},{96,128},{128,160},{160,192},{192,224},{224... | collective-permute-start | bytes 3848 | tf_op jit(solution)/shard_map/ppermute | solution.py:38
  148.7 14.6 %collective-permute-start.19 = (f32[5,8,1,128]{3,2,1,0:T(1,128)S(1)}, f32[5,8,1,128]{3,2,1,0:T(1,128)S(1)}, u32[]{:S(2)}, u32[]{:S(2)}) collective-permute-start(f32[5,8,1,128]{3,2,1,0:T(1,128)S(1)} %get-tuple-element.13), channel_id=1, source_target_pairs={{0,2},{2,4},{4,6},{6,8},{8,10},{10,12},{12,14},{14,16},{16,18},{18... | collective-permute-start | bytes 61448 | tf_op jit(solution)/shard_map/ppermute | solution.py:38
  152.8 10.4 %collective-permute-start.18 = (f32[5,8,1,128]{3,2,1,0:T(1,128)S(1)}, f32[5,8,1,128]{3,2,1,0:T(1,128)S(1)}, u32[]{:S(2)}, u32[]{:S(2)}) collective-permute-start(f32[5,8,1,128]{3,2,1,0:T(1,128)S(1)} %get-tuple-element.14), channel_id=1, source_target_pairs={{2,0},{4,2},{6,4},{8,6},{10,8},{12,10},{14,12},{16,14},{18,16},{20... | collective-permute-start | bytes 61448 | tf_op jit(solution)/shard_map/ppermute | solution.py:39
  158.3 5.2 %collective-permute-start.17 = (f32[5,8,128]{2,1,0:T(8,128)S(1)}, f32[5,8,128]{2,1,0:T(8,128)S(1)}, u32[]{:S(2)}, u32[]{:S(2)}) collective-permute-start(f32[5,8,128]{2,1,0:T(8,128)S(1)} %dynamic-slice_bitcast_fusion), channel_id=1, source_target_pairs={{0,1},{1,0},{2,3},{3,2},{4,5},{5,4},{6,7},{7,6},{8,9},{9,8},{10,11... | collective-permute-start | bytes 61448 | tf_op jit(solution)/shard_map/ppermute | solution.py:28
where the time goes:
time: 166 us; the launch traced here: 165 us
  starting transfers between devices  115 us (69%)
  waiting for transfers between devices  30.6 us (18%)
  local copies, waits for them, and re-layouts  7.99 us (5%)
  between operations  5.95 us (4%)
  other arithmetic  4.57 us (3%)
    ppermute x8, starting transfers between devices, padded(): after = lax.ppermute(leading, axis, down)  46.8 us
    all_to_all x4, starting transfers between devices, sent_to_all(): lax.all_to_all(jnp.broadcast_to(x[None], (count, *x.shape)), axis, 0, 0,...  41.5 us
    ppermute x8, starting transfers between devices, padded(): before = lax.ppermute(last, axis, up)  19 us
    all_to_all x4, waiting for transfers between devices, sent_to_all(): lax.all_to_all(jnp.broadcast_to(x[None], (count, *x.shape)), axis, 0, 0,...  17.8 us
    ppermute x8, waiting for transfers between devices, padded(): before = lax.ppermute(last, axis, up)  11.7 us
    ppermute x4, starting transfers between devices, swapped(): return lax.ppermute(value, axis, pairs)  7.64 us
    broadcast_in_dim x4, local copies, waits for them, and re-layouts, sent_to_all(): jnp.broadcast_to(x[None], (count, *x.shape))  3.5 us
  transfers between devices with their start and end apart: 24, of which 9 were waited for; matrix products, arithmetic and copies ran while one was open for 3% of the time, Pallas kernels for 0%

commit v1 on v0

v1 whole, which is shorter than its diff:
```python
import jax
import jax.numpy as jnp
from jax import lax
from jax.experimental import pallas as pl
from jax.experimental.pallas import tpu as pltpu
from jax.sharding import PartitionSpec as P

NV = 5
CA = 8
AXIAL_MACH = 0.4
STEP = 0.3
F32 = jnp.float32
INTERPRET = False


def call(kernel, out_shape, *args):
    spec = pl.BlockSpec(memory_space=pltpu.VMEM)
    many = isinstance(out_shape, tuple)
    return pl.pallas_call(
        kernel,
        in_specs=[spec] * len(args),
        out_specs=(spec,) * len(out_shape) if many else spec,
        out_shape=out_shape,
        interpret=INTERPRET,
    )(*[pltpu.with_memory_space_constraint(a, pltpu.VMEM) for a in args])


def sds(*shape):
    return pltpu.VMEM(shape, F32)


def lanes():
    return lax.broadcasted_iota(jnp.int32, (8, 128), 1)


def subs():
    return lax.broadcasted_iota(jnp.int32, (8, 128), 0)


def is_even(axis):
    return lax.axis_index(axis) % 2 == 0


def radial_out(state, eddy, inner, outer):
    upper = subs() < 4
    even_rad = is_even("rad")
    for field in range(NV + 1):
        for pair in range(CA // 2):
            if field < NV:
                even, odd = state[field, 2 * pair], state[field, 2 * pair + 1]
            else:
                even, odd = eddy[2 * pair], eddy[2 * pair + 1]
            to_low = jnp.where(upper, even, pltpu.roll(odd, 4, 0))
            to_high = jnp.where(upper, pltpu.roll(even, 4, 0), odd)
            inner[field, pair] = jnp.where(even_rad, to_high, to_low)
            outer[field, pair] = jnp.where(even_rad, to_low, to_high)


def matrices(index, weight, out):
    side = lax.axis_index("ax")
    rows = lax.broadcasted_iota(jnp.int32, (128, 128), 0)
    for section in range(4):
        taps_at = index[side, section]
        weights = weight[side, section]
        weights = weights / jnp.sum(weights, axis=0, keepdims=True)
        total = jnp.zeros((128, 128), F32)
        for tap in range(4):
            total = total + jnp.where(rows == taps_at[tap : tap + 1], weights[tap : tap + 1], 0.0)
        out[section] = total


def send_edges(tiles, inner, outer, half):
    lane = lanes()
    first = jnp.zeros((8, 128), F32)
    last = jnp.zeros((8, 128), F32)
    for var in range(NV):
        for a in range(CA):
            k = var * CA + a
            x = tiles[var][a]
            first = jnp.where(lane == k, pltpu.roll(x, k, 1) if k else x, first)
            last = jnp.where(lane == k, pltpu.roll(x, k + 1, 1), last)
    even = is_even("circ")
    inner[pl.ds(8 * half, 8)] = jnp.where(even, last, first)
    outer[pl.ds(8 * half, 8)] = jnp.where(even, first, last)


def assemble(state, eddy, from_inner, from_outer, ext, eddy_ext, plane, west, east):
    upper = subs() < 4
    is_rotor = lax.axis_index("ax") == 1
    even_rad = is_even("rad")
    tiles = [[], []]
    for field in range(NV + 1):
        own_row, far_row = [], []
        for a in range(CA):
            pair = a // 2
            near, other = from_inner[field, pair], from_outer[field, pair]
            high = jnp.where(even_rad, near, other)
            low = jnp.where(even_rad, other, near)
            if a % 2 == 0:
                far = jnp.where(upper, high, pltpu.roll(low, 4, 0))
            else:
                far = jnp.where(upper, pltpu.roll(high, 4, 0), low)
            own = state[field, a] if field < NV else eddy[a]
            if field < NV:
                ext[field, a, 0:8] = own
                ext[field, a, 8:16] = far
            else:
                eddy_ext[a, 0:8] = own
                eddy_ext[a, 8:16] = far
            own_row.append(own)
            far_row.append(far)
        tiles[0].append(own_row)
        tiles[1].append(far_row)
    for half in range(2):
        for var in range(NV):
            plane[var, pl.ds(8 * half, 8)] = jnp.where(is_rotor, tiles[half][var][0], tiles[half][var][CA - 1])
        send_edges(tiles[half], west, east, half)


def section_body(last, first, refs):
    if last:
        field, base, acc_in, eddy, ghost_in, matrix, from_inner, from_outer, out = refs
    elif first:
        field, eddy, ghost_in, matrix, from_inner, from_outer, nxt, acc_out, plane, west, east = refs
        base = field
    else:
        field, base, acc_in, eddy, ghost_in, matrix, from_inner, from_outer, nxt, acc_out, plane, west, east = refs
    section = refs_section[0]
    lane, sub = lanes(), subs()
    even_circ = is_even("circ")
    is_rotor = lax.axis_index("ax") == 1
    rad = lax.axis_index("rad")
    count = lax.axis_size("rad")
    swirl = jnp.where(is_rotor, F32(-0.3), F32(0.2))
    halves = 1 if last else 2
    ghost = jnp.dot(
        ghost_in[...].reshape(NV * 8 * halves, 128),
        matrix[section],
        precision=lax.Precision.HIGHEST,
        preferred_element_type=F32,
    ).reshape(NV, 8 * halves, 128)
    inside = jnp.where(sub < 4, jnp.where(rad == count - 1, 0.0, 1.0), jnp.where(rad == 0, 0.0, 1.0)).astype(F32)
    step = (0.5 * STEP, 0.5 * STEP, STEP, 0.0)[section]
    gain = STEP / 6.0 * (1.0, 2.0, 2.0, 1.0)[section]
    x = [[[field[v, a, 0:8], field[v, a, 8:16]] for a in range(CA)] for v in range(NV)]
    zero = jnp.zeros((8, 128), F32)
    tiles = [[[None] * CA for _ in range(NV)] for _ in range(2)]
    for half in range(halves):
        near, other = from_inner[pl.ds(8 * half, 8)], from_outer[pl.ds(8 * half, 8)]
        west_msg = jnp.where(even_circ, other, near)
        east_msg = jnp.where(even_circ, near, other)
        for a in range(CA):
            e = eddy[a, pl.ds(8 * half, 8)]
            dc, dr, da, lap = [], [], [], []
            for v in range(NV):
                k = v * CA + a
                c = x[v][a][half]
                o = x[v][a][1 - half]
                cp = jnp.where(lane == 0, pltpu.roll(west_msg, (128 - k) % 128, 1) if k else west_msg, pltpu.roll(c, 1, 1))
                cn = jnp.where(lane == 127, pltpu.roll(east_msg, 127 - k, 1), pltpu.roll(c, 127, 1))
                up = pltpu.roll(jnp.where(sub == 0, o, c), 7, 0)
                dn = pltpu.roll(jnp.where(sub == 7, o, c), 1, 0)
                g = ghost[v, 8 * half : 8 * half + 8]
                lo = x[v][a - 1][half] if a > 0 else jnp.where(is_rotor, g, zero)
                hi = x[v][a + 1][half] if a < CA - 1 else jnp.where(is_rotor, zero, g)
                dc.append(cn - cp)
                dr.append(up - dn)
                da.append(hi - lo)
                lap.append((cn + cp) + (up + dn) + (hi + lo) - 6.0 * c)
            div = 0.5 * (dc[1] + dr[2] + da[3])
            flux = (div, 0.5 * dc[4], 0.5 * dr[4], 0.5 * da[4], div)
            for v in range(NV):
                slope = e * lap[v] - (0.5 * swirl) * dc[v] - (0.5 * AXIAL_MACH) * da[v] - flux[v]
                rows = pl.ds(8 * half, 8)
                if last:
                    out[v, a] = acc_in[v, a] + gain * slope
                    continue
                if half == 1:
                    slope = slope * inside
                u = base[v, a, rows] + step * slope
                nxt[v, a, rows] = u
                tiles[half][v][a] = u
                if half == 0:
                    acc_out[v, a] = (base[v, a, 0:8] if first else acc_in[v, a]) + gain * slope
    if last:
        return
    send_halves = 1 if section == 2 else 2
    for half in range(send_halves):
        for v in range(NV):
            plane[v, pl.ds(8 * half, 8)] = jnp.where(is_rotor, tiles[half][v][0], tiles[half][v][CA - 1])
        send_edges(tiles[half], west, east, half)


refs_section = [0]


def section_call(section, *args):
    last, first = section == 3, section == 0

    def kernel(*refs):
        refs_section[0] = section
        section_body(last, first, refs)

    if last:
        return call(kernel, jax.ShapeDtypeStruct((NV, CA, 8, 128), F32), *args)
    rows = 8 if section == 2 else 16
    shapes = (sds(NV, CA, 16, 128), sds(NV, CA, 8, 128), sds(NV, rows, 128), sds(rows, 128), sds(rows, 128))
    return call(kernel, shapes, *args)


SPECIAL = (0, 16, 31)


def inner_pairs(count):
    return [(i, i ^ 1) for i in range(count)]


def outer_pairs(count, wrap):
    pairs = [(i, i + 1 if i % 2 else i - 1) for i in range(count)]
    return [(i, j % count) for i, j in pairs if wrap or 0 <= j < count]


def facing(plane, offset):
    count = lax.axis_size("circ")
    pairs = [(2 * ((c + offset) % count), 2 * c + 1) for c in range(count)]
    pairs += [(j, i) for i, j in pairs]
    return lax.ppermute(plane, ("circ", "ax"), pairs)


def beside(inner, outer):
    count = lax.axis_size("circ")
    from_outer = lax.ppermute(outer, "circ", outer_pairs(count, True))
    from_inner = lax.ppermute(inner, "circ", inner_pairs(count))
    return from_inner, from_outer


def exchange(kind, place, plane, inner, outer):
    others = [o for o in range(lax.axis_size("circ")) if o not in SPECIAL]

    def special(o):
        return lambda plane, inner, outer: (facing(plane, o), *beside(inner, outer))

    def general(plane, inner, outer):
        sides = beside(inner, outer)
        ghost = lax.switch(place, [lambda p, o=o: facing(p, o) for o in others], plane)
        return (ghost, *sides)

    return lax.switch(kind, [special(o) for o in SPECIAL] + [general], plane, inner, outer)


def local(state, eddy, offsets, stencil_index, stencil_weight):
    index = jnp.transpose(stencil_index, (0, 1, 3, 2))
    weight = jnp.transpose(stencil_weight, (0, 1, 3, 2))
    count = lax.axis_size("rad")
    kind = jnp.where(offsets == 0, 0, jnp.where(offsets == 16, 1, jnp.where(offsets == 31, 2, 3)))
    place = offsets - (offsets > 0).astype(jnp.int32) - (offsets > 16).astype(jnp.int32)
    message = sds(NV + 1, CA // 2, 8, 128)
    inner, outer = call(radial_out, (message, message), state, eddy)
    from_outer = lax.ppermute(outer, "rad", outer_pairs(count, False))
    from_inner = lax.ppermute(inner, "rad", inner_pairs(count))
    matrix = call(matrices, sds(4, 128, 128), index, weight)
    ext, eddy_ext, plane, west, east = call(
        assemble,
        (sds(NV, CA, 16, 128), sds(CA, 16, 128), sds(NV, 16, 128), sds(16, 128), sds(16, 128)),
        state, eddy, from_inner, from_outer,
    )
    ghost, fw, fe = exchange(kind[0], place[0], plane, west, east)
    field, acc, plane, west, east = section_call(0, ext, eddy_ext, ghost, matrix, fw, fe)
    for section in (1, 2):
        ghost, fw, fe = exchange(kind[section], place[section], plane, west, east)
        field, acc, plane, west, east = section_call(section, field, ext, acc, eddy_ext, ghost, matrix, fw, fe)
    ghost, fw, fe = exchange(kind[3], place[3], plane, west, east)
    return section_call(3, field, ext, acc, eddy_ext, ghost, matrix, fw, fe)


def solution(mesh):
    return jax.shard_map(
        local,
        mesh=mesh,
        in_specs=(P(None, "ax", "rad", "circ"), P("ax", "rad", "circ"), P(), P(), P()),
        out_specs=P(None, "ax", "rad", "circ"),
        check_vma=False,
    )
```

time: 166 us -> 97.1 us (0.58)
  the two profiles are of different devices: /device:TPU:48 before, /device:TPU:65 now
where the time goes in v1:
time: 97.1 us; the launch traced here: 96.4 us
  starting transfers between devices  59.1 us (61%)
  waiting for transfers between devices  24.6 us (25%)
  Pallas kernels  6.22 us (6%)
  local copies, waits for them, and re-layouts  3 us (3%)
  between operations  2.61 us (3%)
    ppermute x4, starting transfers between devices, facing(): return lax.ppermute(plane, ('circ', 'ax'), pairs)  33 us
    ppermute x4, waiting for transfers between devices, beside(): from_outer = lax.ppermute(outer, 'circ', outer_pairs(count, True))  15.7 us
    ppermute x4, starting transfers between devices, beside(): from_outer = lax.ppermute(outer, 'circ', outer_pairs(count, True))  12.6 us
    ppermute x4, starting transfers between devices, beside(): from_inner = lax.ppermute(inner, 'circ', inner_pairs(count))  8.35 us
    pallas_call x7, Pallas kernels, call(): pl.pallas_call(kernel, in_specs=[spec] * len(args), out_specs=(spec,) * l...  6.22 us
    ppermute x4, waiting for transfers between devices, facing(): return lax.ppermute(plane, ('circ', 'ax'), pairs)  5.75 us
    ppermute x1, starting transfers between devices, local(): from_inner = lax.ppermute(inner, 'rad', inner_pairs(count))  3.25 us
    ppermute x1, waiting for transfers between devices, local(): from_outer = lax.ppermute(outer, 'rad', outer_pairs(count, False))  2.14 us
  transfers between devices with their start and end apart: 14, of which 6 were waited for; matrix products, arithmetic and copies ran while one was open for 1% of the time, Pallas kernels for 0%

profile of v1, /device:TPU:65, one launch (start us, length us, event | category | flops | bytes accessed | tf_op | source)
XLA Modules:
  0.0 96.4 jit_solution(11705443013465777421)
XLA Ops:
  0.0 0.0 copy-start
  0.0 0.9 copy-done
  0.9 0.0 copy-start.2
  0.9 0.8 copy-done.2
  1.7 0.0 copy-start.5
  1.7 0.0 copy-start.3
  1.7 0.0 copy-start.4
  1.7 0.0 copy-start.1
  1.7 3.3 %collective-permute-start.160 = (f32[6,4,8,128]{3,2,1,0:T(8,128)S(1)}, f32[6,4,8,128]{3,2,1,0:T(8,128)S(1)}, u32[]{:S(2)}, u32[]{:S(2)}) collective-permute-start(f32[6,4,8,128]{3,2,1,0:T(8,128)S(1)} %get-tuple-element.439), channel_id=1, source_target_pairs={{0,2},{2,0},{4,6},{6,4},{8,10},{10,8},{12,14},{14,12},{16,18},{18,... | collective-permute-start | bytes 294920 | tf_op jit(solution)/shard_map/ppermute | solution.py:260
  5.0 1.9 %collective-permute-start.161 = (f32[6,4,8,128]{3,2,1,0:T(8,128)S(1)}, f32[6,4,8,128]{3,2,1,0:T(8,128)S(1)}, u32[]{:S(2)}, u32[]{:S(2)}) collective-permute-start(f32[6,4,8,128]{3,2,1,0:T(8,128)S(1)} %get-tuple-element.440), channel_id=1, source_target_pairs={{2,4},{4,2},{6,8},{8,6},{10,12},{12,10},{14,16},{16,14},{18,20},{2... | collective-permute-start | bytes 294920 | tf_op jit(solution)/shard_map/ppermute | solution.py:259
  6.9 0.0 copy-done.5
  7.0 0.7 fusion.2
  10.1 0.0 copy-done.3
  10.1 0.0 copy-done.4
  10.2 0.2 shard_map.57.refs_3_.refs_5_
  10.3 0.0 collective-permute-done.160.from_inner
  10.3 2.1 %collective-permute-done.161.from_outer = f32[6,4,8,128]{3,2,1,0:T(8,128)S(1)} collective-permute-done((f32[6,4,8,128]{3,2,1,0:T(8,128)S(1)}, f32[6,4,8,128]{3,2,1,0:T(8,128)S(1)}, u32[]{:S(2)}, u32[]{:S(2)}) %collective-permute-start.161) | collective-permute-done | bytes 98336 | tf_op jit(solution)/shard_map/ppermute | solution.py:259
  12.5 0.0 copy-done.1
  12.5 0.2 shard_map.56
  12.7 32.0 %conditional.8 = (f32[5,16,128]{2,1,0:T(8,128)}, f32[16,128]{1,0:T(8,128)}, f32[16,128]{1,0:T(8,128)}) conditional(s32[]{:T(128)} %bitcast.4, (f32[5,16,128]{2,1,0:T(8,128)S(1)}, f32[16,128]{1,0:T(8,128)S(1)}, f32[16,128]{1,0:T(8,128)S(1)}) %tuple.417, (f32[5,16,128]{2,1,0:T(8,128)S(1)}, f32[16,128]{1,0:T(8,128)S(1)}, ...), branch_computations={%region_0.1_spmd, %region_1.2_spmd, %region_2.3_spmd, %region_3.33... | conditional | flops 1 | bytes 229544 | solution.py:248
  12.7 21.3 %collective-permute-start.6 = (f32[5,16,128]{2,1,0:T(8,128)S(1)}, f32[5,16,128]{2,1,0:T(8,128)}, u32[]{:S(2)}, u32[]{:S(2)}) collective-permute-start(f32[5,16,128]{2,1,0:T(8,128)S(1)} %get-tuple-element.359), channel_id=1, source_target_pairs={{992,1},{0,33},{32,65},{64,97},{96,129},{128,161},{160,193},{192,2... | collective-permute-start | bytes 122888 | tf_op jit(solution)/shard_map/cond/branch_2_fun/ppermute | solution.py:227
  34.0 1.9 %collective-permute-start.7 = (f32[16,128]{1,0:T(8,128)S(1)}, f32[16,128]{1,0:T(8,128)}, u32[]{:S(2)}, u32[]{:S(2)}) collective-permute-start(f32[16,128]{1,0:T(8,128)S(1)} %get-tuple-element.360), channel_id=1, source_target_pairs={{0,32},{32,0},{64,96},{96,64},{128,160},{160,128},{192,224},{224,1... | collective-permute-start | bytes 24584 | tf_op jit(solution)/shard_map/cond/branch_2_fun/ppermute | solution.py:233
  36.0 1.9 %collective-permute-start.8 = (f32[16,128]{1,0:T(8,128)S(1)}, f32[16,128]{1,0:T(8,128)}, u32[]{:S(2)}, u32[]{:S(2)}) collective-permute-start(f32[16,128]{1,0:T(8,128)S(1)} %get-tuple-element.361), channel_id=1, source_target_pairs={{0,992},{32,64},{64,32},{96,128},{128,96},{160,192},{192,160},{224... | collective-permute-start | bytes 24584 | tf_op jit(solution)/shard_map/cond/branch_2_fun/ppermute | solution.py:232
  37.9 0.9 collective-permute-done.7
  38.8 5.9 %collective-permute-done.8 = f32[16,128]{1,0:T(8,128)} collective-permute-done((f32[16,128]{1,0:T(8,128)S(1)}, f32[16,128]{1,0:T(8,128)}, u32[]{:S(2)}, u32[]{:S(2)}) %collective-permute-start.8) | collective-permute-done | bytes 8224 | tf_op jit(solution)/shard_map/cond/branch_2_fun/ppermute | solution.py:232
  44.7 0.0 collective-permute-done.6
  44.7 1.4 %shard_map.58 = (f32[5,8,16,128]{3,2,1,0:T(8,128)S(1)}, f32[5,8,8,128]{3,2,1,0:T(8,128)S(1)}, f32[5,16,128]{2,1,0:T(8,128)S(1)}, f32[16,128]{1,0:T(8,128)S(1)}, f32[16,128]{1,0:T(8,128)S(1)}) custom-call(f32[5,8,16,128]{3,2,1,0:T(8,128)S(1)} %get-tuple-element.441.refs_0_.refs_1_, f32[8,16,128]{2,1,0:T(8,128)S(1)} %get-tuple-element.442.refs_1_.refs_3_, ...), custom_call_target="tpu_custom_call" | custom-call | tf_op jit(solution)/shard_map/pallas_call | solution.py:19
  46.1 12.6 %conditional.9 = (f32[5,16,128]{2,1,0:T(8,128)}, f32[16,128]{1,0:T(8,128)}, f32[16,128]{1,0:T(8,128)}) conditional(s32[]{:T(128)} %bitcast.7, (f32[5,16,128]{2,1,0:T(8,128)S(1)}, f32[16,128]{1,0:T(8,128)S(1)}, f32[16,128]{1,0:T(8,128)S(1)}) %tuple.419, (f32[5,16,128]{2,1,0:T(8,128)S(1)}, f32[16,128]{1,0:T(8,128)S(1)}, ...), branch_computations={%region_33.34_spmd, %region_34.35_spmd, %region_35.36_spmd, %regio... | conditional | flops 1 | bytes 229552 | solution.py:248
  46.1 1.9 %collective-permute-start.40 = (f32[5,16,128]{2,1,0:T(8,128)S(1)}, f32[5,16,128]{2,1,0:T(8,128)}, u32[]{:S(2)}, u32[]{:S(2)}) collective-permute-start(f32[5,16,128]{2,1,0:T(8,128)S(1)} %get-tuple-element.366), channel_id=1, source_target_pairs={{0,1},{32,33},{64,65},{96,97},{128,129},{160,161},{192,193},{224,2... | collective-permute-start | bytes 122888 | tf_op jit(solution)/shard_map/cond/branch_0_fun/ppermute | solution.py:227
  48.0 1.9 %collective-permute-start.41 = (f32[16,128]{1,0:T(8,128)S(1)}, f32[16,128]{1,0:T(8,128)}, u32[]{:S(2)}, u32[]{:S(2)}) collective-permute-start(f32[16,128]{1,0:T(8,128)S(1)} %get-tuple-element.367), channel_id=1, source_target_pairs={{0,32},{32,0},{64,96},{96,64},{128,160},{160,128},{192,224},{224,1... | collective-permute-start | bytes 24584 | tf_op jit(solution)/shard_map/cond/branch_0_fun/ppermute | solution.py:233
  50.0 3.2 %collective-permute-start.42 = (f32[16,128]{1,0:T(8,128)S(1)}, f32[16,128]{1,0:T(8,128)}, u32[]{:S(2)}, u32[]{:S(2)}) collective-permute-start(f32[16,128]{1,0:T(8,128)S(1)} %get-tuple-element.368), channel_id=1, source_target_pairs={{0,992},{32,64},{64,32},{96,128},{128,96},{160,192},{192,160},{224... | collective-permute-start | bytes 24584 | tf_op jit(solution)/shard_map/cond/branch_0_fun/ppermute | solution.py:232
  53.2 0.0 collective-permute-done.41
  53.2 5.5 %collective-permute-done.42 = f32[16,128]{1,0:T(8,128)} collective-permute-done((f32[16,128]{1,0:T(8,128)S(1)}, f32[16,128]{1,0:T(8,128)}, u32[]{:S(2)}, u32[]{:S(2)}) %collective-permute-start.42) | collective-permute-done | bytes 8224 | tf_op jit(solution)/shard_map/cond/branch_0_fun/ppermute | solution.py:232
  58.7 0.0 collective-permute-done.40
  58.7 1.4 %shard_map.59 = (f32[5,8,16,128]{3,2,1,0:T(8,128)S(1)}, f32[5,8,8,128]{3,2,1,0:T(8,128)S(1)}, f32[5,16,128]{2,1,0:T(8,128)S(1)}, f32[16,128]{1,0:T(8,128)S(1)}, f32[16,128]{1,0:T(8,128)S(1)}) custom-call(f32[5,8,16,128]{3,2,1,0:T(8,128)S(1)} %get-tuple-element.449.refs_0_, f32[5,8,16,128]{3,2,1,0:T(8,128)S(1)} %get-tuple-element.441.refs_0_.refs_1_, ...), custom_call_target="tpu_custom_call" | custom-call | tf_op jit(solution)/shard_map/pallas_call | solution.py:19
  60.1 14.2 %conditional.10 = (f32[5,16,128]{2,1,0:T(8,128)}, f32[16,128]{1,0:T(8,128)}, f32[16,128]{1,0:T(8,128)}) conditional(s32[]{:T(128)} %bitcast.8, (f32[5,16,128]{2,1,0:T(8,128)S(1)}, f32[16,128]{1,0:T(8,128)S(1)}, f32[16,128]{1,0:T(8,128)S(1)}) %tuple.421, (f32[5,16,128]{2,1,0:T(8,128)S(1)}, f32[16,128]{1,0:T(8,128)S(1)}, ...), branch_computations={%region_66.67_spmd, %region_67.68_spmd, %region_68.69_spmd, %regio... | conditional | flops 1 | bytes 229552 | solution.py:248
  60.1 1.9 %collective-permute-start.118 = (f32[16,128]{1,0:T(8,128)S(1)}, f32[16,128]{1,0:T(8,128)}, u32[]{:S(2)}, u32[]{:S(2)}) collective-permute-start(f32[16,128]{1,0:T(8,128)S(1)} %get-tuple-element.390), channel_id=1, source_target_pairs={{0,32},{32,0},{64,96},{96,64},{128,160},{160,128},{192,224},{224,1... | collective-permute-start | bytes 24584 | tf_op jit(solution)/shard_map/cond/branch_3_fun/ppermute | solution.py:233
  62.0 3.2 %collective-permute-start.119 = (f32[16,128]{1,0:T(8,128)S(1)}, f32[16,128]{1,0:T(8,128)}, u32[]{:S(2)}, u32[]{:S(2)}) collective-permute-start(f32[16,128]{1,0:T(8,128)S(1)} %get-tuple-element.391), channel_id=1, source_target_pairs={{0,992},{32,64},{64,32},{96,128},{128,96},{160,192},{192,160},{224... | collective-permute-start | bytes 24584 | tf_op jit(solution)/shard_map/cond/branch_3_fun/ppermute | solution.py:232
  65.2 0.6 slice.22
  66.6 7.7 %conditional.2 = (f32[5,16,128]{2,1,0:T(8,128)}) conditional(s32[]{:T(128)} %bitcast.2, f32[5,16,128]{2,1,0:T(8,128)S(1)} %get-tuple-element.389, f32[5,16,128]{2,1,0:T(8,128)S(1)} %get-tuple-element.389, f32[5,16,128]{2,1,0:T(8,128)S(1)} %get-tuple-element.389, f32[5,16,128]{2,1,0:T(8,128)S(1)} %get-tuple-element.389, ...), branch_computations={%region_70.70_spmd, %region_71.71_spmd, %region_72.72_spmd, %regio... | conditional | bytes 163888 | solution.py:245
  66.6 1.9 %collective-permute-start.94 = (f32[5,16,128]{2,1,0:T(8,128)S(1)}, f32[5,16,128]{2,1,0:T(8,128)}, u32[]{:S(2)}, u32[]{:S(2)}) collective-permute-start(f32[5,16,128]{2,1,0:T(8,128)S(1)} %param.74), channel_id=1, source_target_pairs={{192,1},{224,33},{256,65},{288,97},{320,129},{352,161},{384,193},{... | collective-permute-start | bytes 122888 | tf_op jit(solution)/shard_map/cond/branch_3_fun/cond/branch_5_fun/ppermute | solution.py:227
  68.5 5.7 %collective-permute-done.94 = f32[5,16,128]{2,1,0:T(8,128)} collective-permute-done((f32[5,16,128]{2,1,0:T(8,128)S(1)}, f32[5,16,128]{2,1,0:T(8,128)}, u32[]{:S(2)}, u32[]{:S(2)}) %collective-permute-start.94) | collective-permute-done | bytes 40992 | tf_op jit(solution)/shard_map/cond/branch_3_fun/cond/branch_5_fun/ppermute | solution.py:227
  74.2 0.0 collective-permute-done.118
  74.3 0.0 collective-permute-done.119
  74.3 1.3 %shard_map.60 = (f32[5,8,16,128]{3,2,1,0:T(8,128)S(1)}, f32[5,8,8,128]{3,2,1,0:T(8,128)S(1)}, f32[5,8,128]{2,1,0:T(8,128)S(1)}, f32[8,128]{1,0:T(8,128)S(1)}, f32[8,128]{1,0:T(8,128)S(1)}) custom-call(f32[5,8,16,128]{3,2,1,0:T(8,128)S(1)} %get-tuple-element.457.refs_0_, f32[5,8,16,128]{3,2,1,0:T(8,128)S(1)} %get-tuple-element.441.refs_0_.refs_1_, ...), custom_call_target="tpu_custom_call" | custom-call | tf_op jit(solution)/shard_map/pallas_call | solution.py:19
  75.6 19.1 %conditional.11 = (f32[5,8,128]{2,1,0:T(8,128)}, f32[8,128]{1,0:T(8,128)}, f32[8,128]{1,0:T(8,128)}) conditional(s32[]{:T(128)} %bitcast.9, (f32[5,8,128]{2,1,0:T(8,128)S(1)}, f32[8,128]{1,0:T(8,128)S(1)}, f32[8,128]{1,0:T(8,128)S(1)}) %tuple.423, (f32[5,8,128]{2,1,0:T(8,128)S(1)}, f32[8,128]{1,0:T(8,128)S(1)}, ...), branch_computations={%region_99.100_spmd, %region_100.101_spmd, %region_101.102_spmd, %... | conditional | flops 1 | bytes 114864 | solution.py:248
  75.6 7.8 %collective-permute-start.123 = (f32[5,8,128]{2,1,0:T(8,128)S(1)}, f32[5,8,128]{2,1,0:T(8,128)}, u32[]{:S(2)}, u32[]{:S(2)}) collective-permute-start(f32[5,8,128]{2,1,0:T(8,128)S(1)} %get-tuple-element.395), channel_id=1, source_target_pairs={{512,1},{544,33},{576,65},{608,97},{640,129},{672,161},{704,193},{... | collective-permute-start | bytes 61448 | tf_op jit(solution)/shard_map/cond/branch_1_fun/ppermute | solution.py:227
  83.4 2.6 %collective-permute-start.124 = (f32[8,128]{1,0:T(8,128)S(1)}, f32[8,128]{1,0:T(8,128)}, u32[]{:S(2)}, u32[]{:S(2)}) collective-permute-start(f32[8,128]{1,0:T(8,128)S(1)} %get-tuple-element.396), channel_id=1, source_target_pairs={{0,32},{32,0},{64,96},{96,64},{128,160},{160,128},{192,224},{224,1... | collective-permute-start | bytes 12296 | tf_op jit(solution)/shard_map/cond/branch_1_fun/ppermute | solution.py:233
  86.0 4.3 %collective-permute-start.125 = (f32[8,128]{1,0:T(8,128)S(1)}, f32[8,128]{1,0:T(8,128)}, u32[]{:S(2)}, u32[]{:S(2)}) collective-permute-start(f32[8,128]{1,0:T(8,128)S(1)} %get-tuple-element.397), channel_id=1, source_target_pairs={{0,992},{32,64},{64,32},{96,128},{128,96},{160,192},{192,160},{224... | collective-permute-start | bytes 12296 | tf_op jit(solution)/shard_map/cond/branch_1_fun/ppermute | solution.py:232
  90.3 0.0 collective-permute-done.124
  90.3 4.4 %collective-permute-done.125 = f32[8,128]{1,0:T(8,128)} collective-permute-done((f32[8,128]{1,0:T(8,128)S(1)}, f32[8,128]{1,0:T(8,128)}, u32[]{:S(2)}, u32[]{:S(2)}) %collective-permute-start.125) | collective-permute-done | bytes 4128 | tf_op jit(solution)/shard_map/cond/branch_1_fun/ppermute | solution.py:232
  94.7 0.0 collective-permute-done.123
  94.7 1.7 %shard_map.61 = f32[5,8,8,128]{3,2,1,0:T(8,128)} custom-call(f32[5,8,16,128]{3,2,1,0:T(8,128)S(1)} %get-tuple-element.465.refs_0_, f32[5,8,16,128]{3,2,1,0:T(8,128)S(1)} %get-tuple-element.441.refs_0_.refs_1_, f32[5,8,8,128]{3,2,1,0:T(8,128)S(1)} %get-tuple-element.466.refs_2_, f32[8,16,128]{2,1,0:T(8,128)S(1)} %get-tuple-element.442.refs_1_.refs_3_, ...), custom_call_target="tpu_custom_call" | custom-call | tf_op jit(solution)/shard_map/pallas_call | solution.py:19
  (2 shorter events, 0.0 us)
Async XLA Ops:
  0.0 0.9 copy-start
  0.9 0.8 copy-start.2
  1.7 5.3 %copy-start.5 = (s32[4]{0:T(128)S(1)}, s32[4]{0:T(128)}, u32[]{:S(2)}) copy-start(s32[4]{0:T(128)} %param.139) | copy-start | bytes 52
  1.7 8.5 %copy-start.3 = (s32[2,4,128,4]{2,3,1,0:T(4,128)S(1)}, s32[2,4,128,4]{2,3,1,0:T(4,128)}, u32[]{:S(2)}) copy-start(s32[2,4,128,4]{2,3,1,0:T(4,128)} %param.140) | copy-start | bytes 49156
  1.7 8.5 %copy-start.4 = (f32[2,4,128,4]{2,3,1,0:T(4,128)S(1)}, f32[2,4,128,4]{2,3,1,0:T(4,128)}, u32[]{:S(2)}) copy-start(f32[2,4,128,4]{2,3,1,0:T(4,128)} %param.141) | copy-start | bytes 49156
  1.7 10.8 %copy-start.1 = (f32[5,8,8,128]{3,2,1,0:T(8,128)S(1)}, f32[5,8,8,128]{3,2,1,0:T(8,128)}, u32[]{:S(2)}) copy-start(f32[5,8,8,128]{3,2,1,0:T(8,128)} %state.3) | copy-start | bytes 491524
  1.7 8.6 %collective-permute-start.160 = (f32[6,4,8,128]{3,2,1,0:T(8,128)S(1)}, f32[6,4,8,128]{3,2,1,0:T(8,128)S(1)}, u32[]{:S(2)}, u32[]{:S(2)}) collective-permute-start(f32[6,4,8,128]{3,2,1,0:T(8,128)S(1)} %get-tuple-element.439), channel_id=1, source_target_pairs={{0,2},{2,0},{4,6},{6,4},{8,10},{10,8},{12,14},{14,12},{16,18},{18,... | collective-permute-start | bytes 294920 | tf_op jit(solution)/shard_map/ppermute | solution.py:260
  5.0 7.5 %collective-permute-start.161 = (f32[6,4,8,128]{3,2,1,0:T(8,128)S(1)}, f32[6,4,8,128]{3,2,1,0:T(8,128)S(1)}, u32[]{:S(2)}, u32[]{:S(2)}) collective-permute-start(f32[6,4,8,128]{3,2,1,0:T(8,128)S(1)} %get-tuple-element.440), channel_id=1, source_target_pairs={{2,4},{4,2},{6,8},{8,6},{10,12},{12,10},{14,16},{16,14},{18,20},{2... | collective-permute-start | bytes 294920 | tf_op jit(solution)/shard_map/ppermute | solution.py:259
  12.7 32.0 %collective-permute-start.6 = (f32[5,16,128]{2,1,0:T(8,128)S(1)}, f32[5,16,128]{2,1,0:T(8,128)}, u32[]{:S(2)}, u32[]{:S(2)}) collective-permute-start(f32[5,16,128]{2,1,0:T(8,128)S(1)} %get-tuple-element.359), channel_id=1, source_target_pairs={{992,1},{0,33},{32,65},{64,97},{96,129},{128,161},{160,193},{192,2... | collective-permute-start | bytes 122888 | tf_op jit(solution)/shard_map/cond/branch_2_fun/ppermute | solution.py:227
  34.0 4.8 %collective-permute-start.7 = (f32[16,128]{1,0:T(8,128)S(1)}, f32[16,128]{1,0:T(8,128)}, u32[]{:S(2)}, u32[]{:S(2)}) collective-permute-start(f32[16,128]{1,0:T(8,128)S(1)} %get-tuple-element.360), channel_id=1, source_target_pairs={{0,32},{32,0},{64,96},{96,64},{128,160},{160,128},{192,224},{224,1... | collective-permute-start | bytes 24584 | tf_op jit(solution)/shard_map/cond/branch_2_fun/ppermute | solution.py:233
  36.0 8.7 %collective-permute-start.8 = (f32[16,128]{1,0:T(8,128)S(1)}, f32[16,128]{1,0:T(8,128)}, u32[]{:S(2)}, u32[]{:S(2)}) collective-permute-start(f32[16,128]{1,0:T(8,128)S(1)} %get-tuple-element.361), channel_id=1, source_target_pairs={{0,992},{32,64},{64,32},{96,128},{128,96},{160,192},{192,160},{224... | collective-permute-start | bytes 24584 | tf_op jit(solution)/shard_map/cond/branch_2_fun/ppermute | solution.py:232
  46.1 12.6 %collective-permute-start.40 = (f32[5,16,128]{2,1,0:T(8,128)S(1)}, f32[5,16,128]{2,1,0:T(8,128)}, u32[]{:S(2)}, u32[]{:S(2)}) collective-permute-start(f32[5,16,128]{2,1,0:T(8,128)S(1)} %get-tuple-element.366), channel_id=1, source_target_pairs={{0,1},{32,33},{64,65},{96,97},{128,129},{160,161},{192,193},{224,2... | collective-permute-start | bytes 122888 | tf_op jit(solution)/shard_map/cond/branch_0_fun/ppermute | solution.py:227
  48.0 5.1 %collective-permute-start.41 = (f32[16,128]{1,0:T(8,128)S(1)}, f32[16,128]{1,0:T(8,128)}, u32[]{:S(2)}, u32[]{:S(2)}) collective-permute-start(f32[16,128]{1,0:T(8,128)S(1)} %get-tuple-element.367), channel_id=1, source_target_pairs={{0,32},{32,0},{64,96},{96,64},{128,160},{160,128},{192,224},{224,1... | collective-permute-start | bytes 24584 | tf_op jit(solution)/shard_map/cond/branch_0_fun/ppermute | solution.py:233
  50.0 8.7 %collective-permute-start.42 = (f32[16,128]{1,0:T(8,128)S(1)}, f32[16,128]{1,0:T(8,128)}, u32[]{:S(2)}, u32[]{:S(2)}) collective-permute-start(f32[16,128]{1,0:T(8,128)S(1)} %get-tuple-element.368), channel_id=1, source_target_pairs={{0,992},{32,64},{64,32},{96,128},{128,96},{160,192},{192,160},{224... | collective-permute-start | bytes 24584 | tf_op jit(solution)/shard_map/cond/branch_0_fun/ppermute | solution.py:232
  60.1 14.1 %collective-permute-start.118 = (f32[16,128]{1,0:T(8,128)S(1)}, f32[16,128]{1,0:T(8,128)}, u32[]{:S(2)}, u32[]{:S(2)}) collective-permute-start(f32[16,128]{1,0:T(8,128)S(1)} %get-tuple-element.390), channel_id=1, source_target_pairs={{0,32},{32,0},{64,96},{96,64},{128,160},{160,128},{192,224},{224,1... | collective-permute-start | bytes 24584 | tf_op jit(solution)/shard_map/cond/branch_3_fun/ppermute | solution.py:233
  62.0 12.2 %collective-permute-start.119 = (f32[16,128]{1,0:T(8,128)S(1)}, f32[16,128]{1,0:T(8,128)}, u32[]{:S(2)}, u32[]{:S(2)}) collective-permute-start(f32[16,128]{1,0:T(8,128)S(1)} %get-tuple-element.391), channel_id=1, source_target_pairs={{0,992},{32,64},{64,32},{96,128},{128,96},{160,192},{192,160},{224... | collective-permute-start | bytes 24584 | tf_op jit(solution)/shard_map/cond/branch_3_fun/ppermute | solution.py:232
  66.6 7.7 %collective-permute-start.94 = (f32[5,16,128]{2,1,0:T(8,128)S(1)}, f32[5,16,128]{2,1,0:T(8,128)}, u32[]{:S(2)}, u32[]{:S(2)}) collective-permute-start(f32[5,16,128]{2,1,0:T(8,128)S(1)} %param.74), channel_id=1, source_target_pairs={{192,1},{224,33},{256,65},{288,97},{320,129},{352,161},{384,193},{... | collective-permute-start | bytes 122888 | tf_op jit(solution)/shard_map/cond/branch_3_fun/cond/branch_5_fun/ppermute | solution.py:227
  75.6 19.1 %collective-permute-start.123 = (f32[5,8,128]{2,1,0:T(8,128)S(1)}, f32[5,8,128]{2,1,0:T(8,128)}, u32[]{:S(2)}, u32[]{:S(2)}) collective-permute-start(f32[5,8,128]{2,1,0:T(8,128)S(1)} %get-tuple-element.395), channel_id=1, source_target_pairs={{512,1},{544,33},{576,65},{608,97},{640,129},{672,161},{704,193},{... | collective-permute-start | bytes 61448 | tf_op jit(solution)/shard_map/cond/branch_1_fun/ppermute | solution.py:227
  83.4 6.9 %collective-permute-start.124 = (f32[8,128]{1,0:T(8,128)S(1)}, f32[8,128]{1,0:T(8,128)}, u32[]{:S(2)}, u32[]{:S(2)}) collective-permute-start(f32[8,128]{1,0:T(8,128)S(1)} %get-tuple-element.396), channel_id=1, source_target_pairs={{0,32},{32,0},{64,96},{96,64},{128,160},{160,128},{192,224},{224,1... | collective-permute-start | bytes 12296 | tf_op jit(solution)/shard_map/cond/branch_1_fun/ppermute | solution.py:233
  86.0 8.7 %collective-permute-start.125 = (f32[8,128]{1,0:T(8,128)S(1)}, f32[8,128]{1,0:T(8,128)}, u32[]{:S(2)}, u32[]{:S(2)}) collective-permute-start(f32[8,128]{1,0:T(8,128)S(1)} %get-tuple-element.397), channel_id=1, source_target_pairs={{0,992},{32,64},{64,32},{96,128},{128,96},{160,192},{192,160},{224... | collective-permute-start | bytes 12296 | tf_op jit(solution)/shard_map/cond/branch_1_fun/ppermute | solution.py:232

commit v2 on v1

v2 whole, which is shorter than its diff:
```python
import jax
import jax.numpy as jnp
from jax import lax
from jax.experimental import pallas as pl
from jax.experimental.pallas import tpu as pltpu
from jax.sharding import PartitionSpec as P

NV = 5
CA = 8
AXIAL_MACH = 0.4
STEP = 0.3
F32 = jnp.float32
INTERPRET = False


def call(kernel, out_shape, *args):
    spec = pl.BlockSpec(memory_space=pltpu.VMEM)
    many = isinstance(out_shape, tuple)
    return pl.pallas_call(
        kernel,
        in_specs=[spec] * len(args),
        out_specs=(spec,) * len(out_shape) if many else spec,
        out_shape=out_shape,
        interpret=INTERPRET,
    )(*[pltpu.with_memory_space_constraint(a, pltpu.VMEM) for a in args])


def sds(*shape):
    return pltpu.VMEM(shape, F32)


def lanes():
    return lax.broadcasted_iota(jnp.int32, (8, 128), 1)


def subs():
    return lax.broadcasted_iota(jnp.int32, (8, 128), 0)


def is_even(axis):
    return lax.axis_index(axis) % 2 == 0


def radial_out(state, eddy, inner, outer):
    upper = subs() < 4
    even_rad = is_even("rad")
    for field in range(NV + 1):
        for pair in range(CA // 2):
            if field < NV:
                even, odd = state[field, 2 * pair], state[field, 2 * pair + 1]
            else:
                even, odd = eddy[2 * pair], eddy[2 * pair + 1]
            to_low = jnp.where(upper, even, pltpu.roll(odd, 4, 0))
            to_high = jnp.where(upper, pltpu.roll(even, 4, 0), odd)
            inner[field, pair] = jnp.where(even_rad, to_high, to_low)
            outer[field, pair] = jnp.where(even_rad, to_low, to_high)


def matrices(index, weight, out):
    side = lax.axis_index("ax")
    rows = lax.broadcasted_iota(jnp.int32, (128, 128), 0)
    for section in range(4):
        taps_at = index[side, section]
        weights = weight[side, section]
        weights = weights / jnp.sum(weights, axis=0, keepdims=True)
        total = jnp.zeros((128, 128), F32)
        for tap in range(4):
            total = total + jnp.where(rows == taps_at[tap : tap + 1], weights[tap : tap + 1], 0.0)
        out[section] = total


def edges_kernel(section):
    def kernel(field, eddy, received, matrix, face, inner, outer):
        lane = lanes()
        even = is_even("circ")
        ghost = interpolated(received, matrix, section)
        face[...] = ghost
        for half in range(2):
            rows = slice(8 * half, 8 * half + 8)
            first = jnp.zeros((8, 128), F32)
            last = jnp.zeros((8, 128), F32)
            for var in range(NV):
                for a in range(CA):
                    k = var * CA + a
                    x = field[var, a, rows]
                    first = place(first, x, 0, k)
                    first = place(first, x, 1, 40 + k)
                    last = place(last, x, 127, k)
                    last = place(last, x, 126, 40 + k)
            for a in range(CA):
                first = place(first, eddy[a, rows], 0, 80 + a)
                last = place(last, eddy[a, rows], 127, 80 + a)
            for var in range(NV):
                for a in (0, CA - 1):
                    k = 88 + var * CA + a
                    first = place(first, ghost[var, rows], 0, k)
                    last = place(last, ghost[var, rows], 127, k)
            inner[rows] = jnp.where(even, last, first)
            outer[rows] = jnp.where(even, first, last)

    return kernel


def turn(x, amount, axis=1):
    amount %= x.shape[axis]
    return pltpu.roll(x, amount, axis) if amount else x


def place(tile, x, source, target):
    return jnp.where(lanes() == target, turn(x, target - source), tile)


def interpolated(received, matrix, section):
    rows = received.shape[1]
    flat = received[...].reshape(NV * rows, 128)
    ghost = jnp.dot(flat, matrix[section], precision=lax.Precision.HIGHEST, preferred_element_type=F32)
    return ghost.reshape(NV, rows, 128)


def side_column(tile, other, own, west, is_rotor, swirl):
    lane, sub = lanes(), subs()
    far = turn(tile, -40)
    low_c, high_c = (far, own) if west else (own, far)
    up = turn(jnp.where(sub == 0, other, tile), 7, 0)
    down = turn(jnp.where(sub == 7, other, tile), 1, 0)
    ghost = turn(tile, -88)
    low = jnp.where(lane % CA == 0, jnp.where(is_rotor, ghost, 0.0), turn(tile, 1))
    high = jnp.where(lane % CA == CA - 1, jnp.where(is_rotor, 0.0, ghost), turn(tile, -1))
    part = jnp.where(lane < CA, turn(tile, -80), 0.0)
    e = part
    for var in range(1, NV):
        e = e + turn(part, CA * var)
    dc, dr, da = high_c - low_c, up - down, high - low
    lap = (high_c + low_c) + (up + down) + (high + low) - 6.0 * tile
    div = turn(dc, -CA) + turn(dr, -2 * CA) + turn(da, -3 * CA)
    flux = turn(div, 4 * CA)
    flux = jnp.where(lane < 4 * CA, turn(da, -CA), flux)
    flux = jnp.where(lane < 3 * CA, turn(dr, -2 * CA), flux)
    flux = jnp.where(lane < 2 * CA, turn(dc, -3 * CA), flux)
    flux = jnp.where(lane < CA, div, flux)
    return e * lap - (0.5 * swirl) * dc - (0.5 * AXIAL_MACH) * da - 0.5 * flux


def assemble(state, eddy, from_inner, from_outer, ext, eddy_ext, plane):
    upper = subs() < 4
    is_rotor = lax.axis_index("ax") == 1
    even_rad = is_even("rad")
    tiles = [[], []]
    for field in range(NV + 1):
        own_row, far_row = [], []
        for a in range(CA):
            pair = a // 2
            near, other = from_inner[field, pair], from_outer[field, pair]
            high = jnp.where(even_rad, near, other)
            low = jnp.where(even_rad, other, near)
            if a % 2 == 0:
                far = jnp.where(upper, high, pltpu.roll(low, 4, 0))
            else:
                far = jnp.where(upper, pltpu.roll(high, 4, 0), low)
            own = state[field, a] if field < NV else eddy[a]
            if field < NV:
                ext[field, a, 0:8] = own
                ext[field, a, 8:16] = far
            else:
                eddy_ext[a, 0:8] = own
                eddy_ext[a, 8:16] = far
            own_row.append(own)
            far_row.append(far)
        tiles[0].append(own_row)
        tiles[1].append(far_row)
    for half in range(2):
        for var in range(NV):
            plane[var, pl.ds(8 * half, 8)] = jnp.where(is_rotor, tiles[half][var][0], tiles[half][var][CA - 1])


def section_kernel(section):
    last, first, paired = section == 3, section == 0, section % 2 == 0

    def kernel(*refs):
        refs = list(refs)
        field = refs.pop(0)
        base = field if first else refs.pop(0)
        acc_in = None if first else refs.pop(0)
        eddy = refs.pop(0)
        if paired:
            face, own_inner, own_outer, from_inner, from_outer = refs[:5]
            refs = refs[5:]
            start_inner, start_outer = (from_inner, from_outer) if first else (refs.pop(0), refs.pop(0))
            ghost = face[...]
        else:
            received, matrix, sides_in = refs[:3]
            refs = refs[3:]
            ghost = interpolated(received, matrix, section)
        if last:
            (out,) = refs
        elif paired:
            nxt, acc_out, plane, sides = refs
        else:
            nxt, acc_out, plane = refs
        lane, sub = lanes(), subs()
        even = is_even("circ")
        is_rotor = lax.axis_index("ax") == 1
        rad = lax.axis_index("rad")
        count = lax.axis_size("rad")
        swirl = jnp.where(is_rotor, F32(-0.3), F32(0.2))
        inside = jnp.where(sub < 4, jnp.where(rad == count - 1, 0.0, 1.0), jnp.where(rad == 0, 0.0, 1.0)).astype(F32)
        step = (0.5 * STEP, 0.5 * STEP, STEP, 0.0)[section]
        gain = STEP / 6.0 * (1.0, 2.0, 2.0, 1.0)[section]
        send_halves = {0: 2, 1: 2, 2: 1, 3: 0}[section]
        zero = jnp.zeros((8, 128), F32)

        def tile(v, a, half):
            return field[v, a, 8 * half : 8 * half + 8]

        def pick(near, beyond, half):
            rows = slice(8 * half, 8 * half + 8)
            x, y = near[rows], beyond[rows]
            return jnp.where(even, y, x), jnp.where(even, x, y)

        for half in range(1 if last else 2):
            rows = slice(8 * half, 8 * half + 8)
            if paired:
                west, east = pick(from_inner, from_outer, half)
            else:
                west, east = sides_in[0, rows], sides_in[1, rows]
            if paired and half < send_halves:
                other_west, other_east = pick(from_inner, from_outer, 1 - half)
                own_last, own_first = pick(own_outer, own_inner, half)
                base_west, base_east = pick(start_inner, start_outer, half)
                for n, (beside, beyond, own, old) in enumerate(
                    ((west, other_west, own_first, base_west), (east, other_east, own_last, base_east))
                ):
                    slope = side_column(beside, beyond, own, n == 0, is_rotor, swirl)
                    if half == 1:
                        slope = slope * inside
                    sides[n, rows] = old + step * slope
            for a in range(CA):
                e = eddy[a, rows]
                dc, dr, da, lap = [], [], [], []
                for v in range(NV):
                    k = v * CA + a
                    c = tile(v, a, half)
                    o = tile(v, a, 1 - half)
                    cp = jnp.where(lane == 0, turn(west, -k), turn(c, 1))
                    cn = jnp.where(lane == 127, turn(east, 127 - k), turn(c, -1))
                    up = turn(jnp.where(sub == 0, o, c), 7, 0)
                    dn = turn(jnp.where(sub == 7, o, c), 1, 0)
                    g = ghost[v, rows]
                    lo = tile(v, a - 1, half) if a > 0 else jnp.where(is_rotor, g, zero)
                    hi = tile(v, a + 1, half) if a < CA - 1 else jnp.where(is_rotor, zero, g)
                    dc.append(cn - cp)
                    dr.append(up - dn)
                    da.append(hi - lo)
                    lap.append((cn + cp) + (up + dn) + (hi + lo) - 6.0 * c)
                div = 0.5 * (dc[1] + dr[2] + da[3])
                flux = (div, 0.5 * dc[4], 0.5 * dr[4], 0.5 * da[4], div)
                for v in range(NV):
                    slope = e * lap[v] - (0.5 * swirl) * dc[v] - (0.5 * AXIAL_MACH) * da[v] - flux[v]
                    if last:
                        out[v, a] = acc_in[v, a] + gain * slope
                        continue
                    if half == 1:
                        slope = slope * inside
                    u = base[v, a, rows] + step * slope
                    nxt[v, a, rows] = u
                    if half == 0:
                        acc_out[v, a] = (base[v, a, 0:8] if first else acc_in[v, a]) + gain * slope
            if half < send_halves:
                for v in range(NV):
                    plane[v, rows] = jnp.where(is_rotor, nxt[v, 0, rows], nxt[v, CA - 1, rows])

    return kernel


def section_call(section, *args):
    if section == 3:
        return call(section_kernel(3), jax.ShapeDtypeStruct((NV, CA, 8, 128), F32), *args)
    rows = 8 if section == 2 else 16
    shapes = (sds(NV, CA, 16, 128), sds(NV, CA, 8, 128), sds(NV, rows, 128))
    if section != 1:
        shapes += (sds(2, rows, 128),)
    return call(section_kernel(section), shapes, *args)


def inner_pairs(count):
    return [(i, i ^ 1) for i in range(count)]


def outer_pairs(count, wrap):
    pairs = [(i, i + 1 if i % 2 else i - 1) for i in range(count)]
    return [(i, j % count) for i, j in pairs if wrap or 0 <= j < count]


def same(source, out):
    out[...] = source[...]


def facing(plane, offset):
    count = lax.axis_size("circ")
    pairs = [(2 * ((c + offset) % count), 2 * c + 1) for c in range(count)]
    pairs += [(j, i) for i, j in pairs]
    ghost = lax.ppermute(plane, ("circ", "ax"), pairs)
    return call(same, sds(*ghost.shape), ghost)


def ghost_of(offset, plane):
    count = lax.axis_size("circ")
    return lax.switch(offset, [lambda p, o=o: facing(p, o) for o in range(count)], plane)


def beside(section, field, eddy, received, matrix):
    count = lax.axis_size("circ")
    shapes = (sds(NV, 16, 128), sds(16, 128), sds(16, 128))
    face, inner, outer = call(edges_kernel(section), shapes, field, eddy, received, matrix)
    from_outer = lax.ppermute(outer, "circ", outer_pairs(count, True))
    from_inner = lax.ppermute(inner, "circ", inner_pairs(count))
    return face, inner, outer, from_inner, from_outer


def local(state, eddy, offsets, stencil_index, stencil_weight):
    index = jnp.transpose(stencil_index, (0, 1, 3, 2))
    weight = jnp.transpose(stencil_weight, (0, 1, 3, 2))
    count = lax.axis_size("rad")
    message = sds(NV + 1, CA // 2, 8, 128)
    inner, outer = call(radial_out, (message, message), state, eddy)
    from_outer = lax.ppermute(outer, "rad", outer_pairs(count, False))
    from_inner = lax.ppermute(inner, "rad", inner_pairs(count))
    matrix = call(matrices, sds(4, 128, 128), index, weight)
    places = [offsets[section] for section in range(4)]
    from_inner, from_outer, matrix, *places = lax.optimization_barrier((from_inner, from_outer, matrix, *places))
    ext, eddy_ext, plane = call(
        assemble,
        (sds(NV, CA, 16, 128), sds(CA, 16, 128), sds(NV, 16, 128)),
        state, eddy, from_inner, from_outer,
    )
    received = ghost_of(places[0], plane)
    edges = beside(0, ext, eddy_ext, received, matrix)
    field, acc, plane, sides = section_call(0, ext, eddy_ext, *edges)
    received = ghost_of(places[1], plane)
    field, acc, plane = section_call(1, field, ext, acc, eddy_ext, received, matrix, sides)
    received = ghost_of(places[2], plane)
    later = beside(2, field, eddy_ext, received, matrix)
    field, acc, plane, sides = section_call(2, field, ext, acc, eddy_ext, *later, *edges[3:])
    received = ghost_of(places[3], plane)
    return section_call(3, field, ext, acc, eddy_ext, received, matrix, sides)


def solution(mesh):
    return jax.shard_map(
        local,
        mesh=mesh,
        in_specs=(P(None, "ax", "rad", "circ"), P("ax", "rad", "circ"), P(), P(), P()),
        out_specs=P(None, "ax", "rad", "circ"),
        check_vma=False,
    )
```

time: 97.1 us -> 85.5 us (0.88)
  the two profiles are of different devices: /device:TPU:65 before, /device:TPU:50 now
where the time goes in v2:
time: 85.5 us; the launch traced here: 84 us
  starting transfers between devices  53.8 us (63%)
  waiting for transfers between devices  20.6 us (24%)
  Pallas kernels  3.79 us (4%)
  local copies, waits for them, and re-layouts  2.84 us (3%)
  between operations  2.74 us (3%)
    ppermute x2, starting transfers between devices, beside(): from_outer = lax.ppermute(outer, 'circ', outer_pairs(count, True))  27.8 us
    ppermute x4, waiting for transfers between devices, facing(): ghost = lax.ppermute(plane, ('circ', 'ax'), pairs)  16.1 us
    ppermute x4, starting transfers between devices, facing(): ghost = lax.ppermute(plane, ('circ', 'ax'), pairs)  10.6 us
    ppermute x2, starting transfers between devices, beside(): from_inner = lax.ppermute(inner, 'circ', inner_pairs(count))  7.11 us
    ppermute x1, starting transfers between devices, local(): from_outer = lax.ppermute(outer, 'rad', outer_pairs(count, False))  5.74 us
    pallas_call x13, Pallas kernels, call(): pl.pallas_call(kernel, in_specs=[spec] * len(args), out_specs=(spec,) * l...  3.79 us
    ppermute x2, waiting for transfers between devices, beside(): from_outer = lax.ppermute(outer, 'circ', outer_pairs(count, True))  3.04 us
    ppermute x1, starting transfers between devices, local(): from_inner = lax.ppermute(inner, 'rad', inner_pairs(count))  2.57 us
  transfers between devices with their start and end apart: 10, of which 7 were waited for; matrix products, arithmetic and copies ran while one was open for 1% of the time, Pallas kernels for 0%

profile of v2, /device:TPU:50, one launch (start us, length us, event | category | flops | bytes accessed | tf_op | source)
XLA Modules:
  0.0 84.0 jit_solution(12785008694919925452)
XLA Ops:
  0.0 0.0 copy-start
  0.0 0.9 %copy-done = f32[5,8,8,128]{3,2,1,0:T(8,128)S(1)} copy-done((f32[5,8,8,128]{3,2,1,0:T(8,128)S(1)}, f32[5,8,8,128]{3,2,1,0:T(8,128)}, u32[]{:S(2)}) %copy-start) | copy-done | bytes 163864
  0.9 0.0 copy-start.2
  0.9 0.8 copy-done.2
  1.7 0.0 copy-start.3
  1.7 0.0 copy-start.4
  1.7 0.0 copy-start.1
  1.7 2.6 %collective-permute-start.128 = (f32[6,4,8,128]{3,2,1,0:T(8,128)S(1)}, f32[6,4,8,128]{3,2,1,0:T(8,128)S(1)}, u32[]{:S(2)}, u32[]{:S(2)}) collective-permute-start(f32[6,4,8,128]{3,2,1,0:T(8,128)S(1)} %get-tuple-element.294), channel_id=1, source_target_pairs={{0,2},{2,0},{4,6},{6,4},{8,10},{10,8},{12,14},{14,12},{16,18},{18,... | collective-permute-start | bytes 294920 | tf_op jit(solution)/shard_map/ppermute | solution.py:327
  4.3 5.7 %collective-permute-start.129 = (f32[6,4,8,128]{3,2,1,0:T(8,128)S(1)}, f32[6,4,8,128]{3,2,1,0:T(8,128)S(1)}, u32[]{:S(2)}, u32[]{:S(2)}) collective-permute-start(f32[6,4,8,128]{3,2,1,0:T(8,128)S(1)} %get-tuple-element.295), channel_id=1, source_target_pairs={{2,4},{4,2},{6,8},{8,6},{10,12},{12,10},{14,16},{16,14},{18,20},{2... | collective-permute-start | bytes 294920 | tf_op jit(solution)/shard_map/ppermute | solution.py:326
  10.1 0.0 copy-done.3
  10.1 0.0 copy-done.4
  10.1 0.0 copy-start.5
  10.1 0.2 shard_map.56.matrix.refs_5_
  10.3 0.5 copy-done.5
  10.7 0.7 fusion
  11.4 0.0 collective-permute-done.128.from_inner
  11.4 1.5 %collective-permute-done.129.from_outer = f32[6,4,8,128]{3,2,1,0:T(8,128)S(1)} collective-permute-done((f32[6,4,8,128]{3,2,1,0:T(8,128)S(1)}, f32[6,4,8,128]{3,2,1,0:T(8,128)S(1)}, u32[]{:S(2)}, u32[]{:S(2)}) %collective-permute-start.129) | collective-permute-done | bytes 98336 | tf_op jit(solution)/shard_map/ppermute | solution.py:326
  12.9 0.0 copy-done.1
  13.6 5.4 %conditional.4 = (f32[5,16,128]{2,1,0:T(8,128)S(1)}) conditional(s32[]{:T(128)} %clamp.12, f32[5,16,128]{2,1,0:T(8,128)S(1)} %get-tuple-element.301, f32[5,16,128]{2,1,0:T(8,128)S(1)} %get-tuple-element.301, f32[5,16,128]{2,1,0:T(8,128)S(1)} %get-tuple-element.301, f32[5,16,128]{2,1,0:T(8,128)S(1)} %get-tuple-element.301, ...), branch_computations={%region_0.0_spmd, %region_1.0_spmd, %region_2.0_spmd, %region_3.0_... | conditional | bytes 163888 | solution.py:308
  13.7 3.4 %collective-permute-start.31 = (f32[5,16,128]{2,1,0:T(8,128)S(1)}, f32[5,16,128]{2,1,0:T(8,128)S(1)}, u32[]{:S(2)}, u32[]{:S(2)}) collective-permute-start(f32[5,16,128]{2,1,0:T(8,128)S(1)} %param.31), channel_id=1, source_target_pairs={{992,1},{0,33},{32,65},{64,97},{96,129},{128,161},{160,193},{192,2... | collective-permute-start | bytes 122888 | tf_op jit(solution)/shard_map/cond/branch_31_fun/ppermute | solution.py:302
  17.1 1.9 %collective-permute-done.31.source = f32[5,16,128]{2,1,0:T(8,128)S(1)} collective-permute-done((f32[5,16,128]{2,1,0:T(8,128)S(1)}, f32[5,16,128]{2,1,0:T(8,128)S(1)}, u32[]{:S(2)}, u32[]{:S(2)}) %collective-permute-start.31) | collective-permute-done | bytes 40992 | tf_op jit(solution)/shard_map/cond/branch_31_fun/ppermute | solution.py:302
  19.0 0.5 shard_map.58
  19.5 5.2 %collective-permute-start.130 = (f32[16,128]{1,0:T(8,128)S(1)}, f32[16,128]{1,0:T(8,128)S(1)}, u32[]{:S(2)}, u32[]{:S(2)}) collective-permute-start(f32[16,128]{1,0:T(8,128)S(1)} %get-tuple-element.304.refs_3_), channel_id=1, source_target_pairs={{0,32},{32,0},{64,96},{96,64},{128,160},{160,128},{192,224},{224,1... | collective-permute-start | bytes 24584 | tf_op jit(solution)/shard_map/ppermute | solution.py:316
  24.7 21.4 %collective-permute-start.131 = (f32[16,128]{1,0:T(8,128)S(1)}, f32[16,128]{1,0:T(8,128)S(1)}, u32[]{:S(2)}, u32[]{:S(2)}) collective-permute-start(f32[16,128]{1,0:T(8,128)S(1)} %get-tuple-element.305.refs_4_), channel_id=1, source_target_pairs={{0,992},{32,64},{64,32},{96,128},{128,96},{160,192},{192,160},{224... | collective-permute-start | bytes 24584 | tf_op jit(solution)/shard_map/ppermute | solution.py:315
  47.5 0.0 collective-permute-done.130.refs_5_.refs_9_
  47.5 0.3 collective-permute-done.131.refs_6_.refs_10_
  47.8 0.7 shard_map.59
  48.5 3.2 %conditional.5 = (f32[5,16,128]{2,1,0:T(8,128)S(1)}) conditional(s32[]{:T(128)} %clamp.13, f32[5,16,128]{2,1,0:T(8,128)S(1)} %get-tuple-element.309, f32[5,16,128]{2,1,0:T(8,128)S(1)} %get-tuple-element.309, f32[5,16,128]{2,1,0:T(8,128)S(1)} %get-tuple-element.309, f32[5,16,128]{2,1,0:T(8,128)S(1)} %get-tuple-element.309, ...), branch_computations={%region_32.0_spmd, %region_33.0_spmd, %region_34.0_spmd, %region_3... | conditional | bytes 163888 | solution.py:308
  48.5 1.9 %collective-permute-start.32 = (f32[5,16,128]{2,1,0:T(8,128)S(1)}, f32[5,16,128]{2,1,0:T(8,128)S(1)}, u32[]{:S(2)}, u32[]{:S(2)}) collective-permute-start(f32[5,16,128]{2,1,0:T(8,128)S(1)} %param.32), channel_id=1, source_target_pairs={{0,1},{32,33},{64,65},{96,97},{128,129},{160,161},{192,193},{224,2... | collective-permute-start | bytes 122888 | tf_op jit(solution)/shard_map/cond/branch_0_fun/ppermute | solution.py:302
  50.5 1.2 %collective-permute-done.32.source = f32[5,16,128]{2,1,0:T(8,128)S(1)} collective-permute-done((f32[5,16,128]{2,1,0:T(8,128)S(1)}, f32[5,16,128]{2,1,0:T(8,128)S(1)}, u32[]{:S(2)}, u32[]{:S(2)}) %collective-permute-start.32) | collective-permute-done | bytes 40992 | tf_op jit(solution)/shard_map/cond/branch_0_fun/ppermute | solution.py:302
  51.7 0.4 shard_map.60
  52.1 9.3 %conditional.6 = (f32[5,16,128]{2,1,0:T(8,128)S(1)}) conditional(s32[]{:T(128)} %clamp.14, f32[5,16,128]{2,1,0:T(8,128)S(1)} %get-tuple-element.314, f32[5,16,128]{2,1,0:T(8,128)S(1)} %get-tuple-element.314, f32[5,16,128]{2,1,0:T(8,128)S(1)} %get-tuple-element.314, f32[5,16,128]{2,1,0:T(8,128)S(1)} %get-tuple-element.314, ...), branch_computations={%region_64.0_spmd, %region_65.0_spmd, %region_66.0_spmd, %region_6... | conditional | bytes 163888 | solution.py:308
  52.2 1.9 %collective-permute-start.70 = (f32[5,16,128]{2,1,0:T(8,128)S(1)}, f32[5,16,128]{2,1,0:T(8,128)S(1)}, u32[]{:S(2)}, u32[]{:S(2)}) collective-permute-start(f32[5,16,128]{2,1,0:T(8,128)S(1)} %param.70), channel_id=1, source_target_pairs={{192,1},{224,33},{256,65},{288,97},{320,129},{352,161},{384,193},{... | collective-permute-start | bytes 122888 | tf_op jit(solution)/shard_map/cond/branch_6_fun/ppermute | solution.py:302
  54.1 7.3 %collective-permute-done.70.source = f32[5,16,128]{2,1,0:T(8,128)S(1)} collective-permute-done((f32[5,16,128]{2,1,0:T(8,128)S(1)}, f32[5,16,128]{2,1,0:T(8,128)S(1)}, u32[]{:S(2)}, u32[]{:S(2)}) %collective-permute-start.70) | collective-permute-done | bytes 40992 | tf_op jit(solution)/shard_map/cond/branch_6_fun/ppermute | solution.py:302
  61.4 0.5 shard_map.61
  61.9 1.9 %collective-permute-start.132 = (f32[16,128]{1,0:T(8,128)S(1)}, f32[16,128]{1,0:T(8,128)S(1)}, u32[]{:S(2)}, u32[]{:S(2)}) collective-permute-start(f32[16,128]{1,0:T(8,128)S(1)} %get-tuple-element.316.refs_5_), channel_id=1, source_target_pairs={{0,32},{32,0},{64,96},{96,64},{128,160},{160,128},{192,224},{224,1... | collective-permute-start | bytes 24584 | tf_op jit(solution)/shard_map/ppermute | solution.py:316
  63.8 6.3 %collective-permute-start.133 = (f32[16,128]{1,0:T(8,128)S(1)}, f32[16,128]{1,0:T(8,128)S(1)}, u32[]{:S(2)}, u32[]{:S(2)}) collective-permute-start(f32[16,128]{1,0:T(8,128)S(1)} %get-tuple-element.317.refs_6_), channel_id=1, source_target_pairs={{0,992},{32,64},{64,32},{96,128},{128,96},{160,192},{192,160},{224... | collective-permute-start | bytes 24584 | tf_op jit(solution)/shard_map/ppermute | solution.py:315
  70.8 0.0 collective-permute-done.132.refs_7_
  70.8 2.8 %collective-permute-done.133.refs_8_ = f32[16,128]{1,0:T(8,128)S(1)} collective-permute-done((f32[16,128]{1,0:T(8,128)S(1)}, f32[16,128]{1,0:T(8,128)S(1)}, u32[]{:S(2)}, u32[]{:S(2)}) %collective-permute-start.133) | collective-permute-done | bytes 8224 | tf_op jit(solution)/shard_map/ppermute | solution.py:315
  73.6 0.5 shard_map.62
  74.0 9.1 %conditional.7 = (f32[5,8,128]{2,1,0:T(8,128)S(1)}) conditional(s32[]{:T(128)} %clamp.15, f32[5,8,128]{2,1,0:T(8,128)S(1)} %get-tuple-element.321, f32[5,8,128]{2,1,0:T(8,128)S(1)} %get-tuple-element.321, f32[5,8,128]{2,1,0:T(8,128)S(1)} %get-tuple-element.321, f32[5,8,128]{2,1,0:T(8,128)S(1)} %get-tuple-element.321, ...), branch_computations={%region_96.0_spmd, %region_97.0_spmd, %region_98.0_spmd, %region_9... | conditional | bytes 81968 | solution.py:308
  74.1 3.3 %collective-permute-start.112 = (f32[5,8,128]{2,1,0:T(8,128)S(1)}, f32[5,8,128]{2,1,0:T(8,128)S(1)}, u32[]{:S(2)}, u32[]{:S(2)}) collective-permute-start(f32[5,8,128]{2,1,0:T(8,128)S(1)} %param.112), channel_id=1, source_target_pairs={{512,1},{544,33},{576,65},{608,97},{640,129},{672,161},{704,193},{... | collective-permute-start | bytes 61448 | tf_op jit(solution)/shard_map/cond/branch_16_fun/ppermute | solution.py:302
  77.4 5.7 %collective-permute-done.112.source = f32[5,8,128]{2,1,0:T(8,128)S(1)} collective-permute-done((f32[5,8,128]{2,1,0:T(8,128)S(1)}, f32[5,8,128]{2,1,0:T(8,128)S(1)}, u32[]{:S(2)}, u32[]{:S(2)}) %collective-permute-start.112) | collective-permute-done | bytes 20512 | tf_op jit(solution)/shard_map/cond/branch_16_fun/ppermute | solution.py:302
  83.1 0.9 %shard_map.63 = f32[5,8,8,128]{3,2,1,0:T(8,128)} custom-call(f32[5,8,16,128]{3,2,1,0:T(8,128)S(1)} %get-tuple-element.318.refs_0_, f32[5,8,16,128]{3,2,1,0:T(8,128)S(1)} %get-tuple-element.298.field.refs_0_.refs_1_, f32[5,8,8,128]{3,2,1,0:T(8,128)S(1)} %get-tuple-element.319.refs_2_, f32[8,16,128]{2,1,0:T(8,128)S(1)} %get-tuple-element.299.eddy.refs_1_.refs_3_, ...), custom_call_target="tpu_custom_call" | custom-call | tf_op jit(solution)/shard_map/pallas_call | solution.py:19
  (6 shorter events, 0.1 us)
Async XLA Ops:
  0.0 0.9 %copy-start = (f32[5,8,8,128]{3,2,1,0:T(8,128)S(1)}, f32[5,8,8,128]{3,2,1,0:T(8,128)}, u32[]{:S(2)}) copy-start(f32[5,8,8,128]{3,2,1,0:T(8,128)} %state.3) | copy-start | bytes 491524
  0.9 0.8 copy-start.2
  1.7 8.4 %copy-start.3 = (s32[2,4,128,4]{2,3,1,0:T(4,128)S(1)}, s32[2,4,128,4]{2,3,1,0:T(4,128)}, u32[]{:S(2)}) copy-start(s32[2,4,128,4]{2,3,1,0:T(4,128)} %param.136) | copy-start | bytes 49156
  1.7 8.4 %copy-start.4 = (f32[2,4,128,4]{2,3,1,0:T(4,128)S(1)}, f32[2,4,128,4]{2,3,1,0:T(4,128)}, u32[]{:S(2)}) copy-start(f32[2,4,128,4]{2,3,1,0:T(4,128)} %param.137) | copy-start | bytes 49156
  1.7 11.2 %copy-start.1 = (f32[5,8,8,128]{3,2,1,0:T(8,128)S(1)}, f32[5,8,8,128]{3,2,1,0:T(8,128)}, u32[]{:S(2)}) copy-start(f32[5,8,8,128]{3,2,1,0:T(8,128)} %state.3) | copy-start | bytes 491524
  1.7 9.7 %collective-permute-start.128 = (f32[6,4,8,128]{3,2,1,0:T(8,128)S(1)}, f32[6,4,8,128]{3,2,1,0:T(8,128)S(1)}, u32[]{:S(2)}, u32[]{:S(2)}) collective-permute-start(f32[6,4,8,128]{3,2,1,0:T(8,128)S(1)} %get-tuple-element.294), channel_id=1, source_target_pairs={{0,2},{2,0},{4,6},{6,4},{8,10},{10,8},{12,14},{14,12},{16,18},{18,... | collective-permute-start | bytes 294920 | tf_op jit(solution)/shard_map/ppermute | solution.py:327
  4.3 8.6 %collective-permute-start.129 = (f32[6,4,8,128]{3,2,1,0:T(8,128)S(1)}, f32[6,4,8,128]{3,2,1,0:T(8,128)S(1)}, u32[]{:S(2)}, u32[]{:S(2)}) collective-permute-start(f32[6,4,8,128]{3,2,1,0:T(8,128)S(1)} %get-tuple-element.295), channel_id=1, source_target_pairs={{2,4},{4,2},{6,8},{8,6},{10,12},{12,10},{14,16},{16,14},{18,20},{2... | collective-permute-start | bytes 294920 | tf_op jit(solution)/shard_map/ppermute | solution.py:326
  10.1 0.7 copy-start.5
  13.7 5.3 %collective-permute-start.31 = (f32[5,16,128]{2,1,0:T(8,128)S(1)}, f32[5,16,128]{2,1,0:T(8,128)S(1)}, u32[]{:S(2)}, u32[]{:S(2)}) collective-permute-start(f32[5,16,128]{2,1,0:T(8,128)S(1)} %param.31), channel_id=1, source_target_pairs={{992,1},{0,33},{32,65},{64,97},{96,129},{128,161},{160,193},{192,2... | collective-permute-start | bytes 122888 | tf_op jit(solution)/shard_map/cond/branch_31_fun/ppermute | solution.py:302
  19.5 28.0 %collective-permute-start.130 = (f32[16,128]{1,0:T(8,128)S(1)}, f32[16,128]{1,0:T(8,128)S(1)}, u32[]{:S(2)}, u32[]{:S(2)}) collective-permute-start(f32[16,128]{1,0:T(8,128)S(1)} %get-tuple-element.304.refs_3_), channel_id=1, source_target_pairs={{0,32},{32,0},{64,96},{96,64},{128,160},{160,128},{192,224},{224,1... | collective-permute-start | bytes 24584 | tf_op jit(solution)/shard_map/ppermute | solution.py:316
  24.7 23.1 %collective-permute-start.131 = (f32[16,128]{1,0:T(8,128)S(1)}, f32[16,128]{1,0:T(8,128)S(1)}, u32[]{:S(2)}, u32[]{:S(2)}) collective-permute-start(f32[16,128]{1,0:T(8,128)S(1)} %get-tuple-element.305.refs_4_), channel_id=1, source_target_pairs={{0,992},{32,64},{64,32},{96,128},{128,96},{160,192},{192,160},{224... | collective-permute-start | bytes 24584 | tf_op jit(solution)/shard_map/ppermute | solution.py:315
  48.5 3.1 %collective-permute-start.32 = (f32[5,16,128]{2,1,0:T(8,128)S(1)}, f32[5,16,128]{2,1,0:T(8,128)S(1)}, u32[]{:S(2)}, u32[]{:S(2)}) collective-permute-start(f32[5,16,128]{2,1,0:T(8,128)S(1)} %param.32), channel_id=1, source_target_pairs={{0,1},{32,33},{64,65},{96,97},{128,129},{160,161},{192,193},{224,2... | collective-permute-start | bytes 122888 | tf_op jit(solution)/shard_map/cond/branch_0_fun/ppermute | solution.py:302
  52.2 9.2 %collective-permute-start.70 = (f32[5,16,128]{2,1,0:T(8,128)S(1)}, f32[5,16,128]{2,1,0:T(8,128)S(1)}, u32[]{:S(2)}, u32[]{:S(2)}) collective-permute-start(f32[5,16,128]{2,1,0:T(8,128)S(1)} %param.70), channel_id=1, source_target_pairs={{192,1},{224,33},{256,65},{288,97},{320,129},{352,161},{384,193},{... | collective-permute-start | bytes 122888 | tf_op jit(solution)/shard_map/cond/branch_6_fun/ppermute | solution.py:302
  61.9 8.9 %collective-permute-start.132 = (f32[16,128]{1,0:T(8,128)S(1)}, f32[16,128]{1,0:T(8,128)S(1)}, u32[]{:S(2)}, u32[]{:S(2)}) collective-permute-start(f32[16,128]{1,0:T(8,128)S(1)} %get-tuple-element.316.refs_5_), channel_id=1, source_target_pairs={{0,32},{32,0},{64,96},{96,64},{128,160},{160,128},{192,224},{224,1... | collective-permute-start | bytes 24584 | tf_op jit(solution)/shard_map/ppermute | solution.py:316
  63.8 9.8 %collective-permute-start.133 = (f32[16,128]{1,0:T(8,128)S(1)}, f32[16,128]{1,0:T(8,128)S(1)}, u32[]{:S(2)}, u32[]{:S(2)}) collective-permute-start(f32[16,128]{1,0:T(8,128)S(1)} %get-tuple-element.317.refs_6_), channel_id=1, source_target_pairs={{0,992},{32,64},{64,32},{96,128},{128,96},{160,192},{192,160},{224... | collective-permute-start | bytes 24584 | tf_op jit(solution)/shard_map/ppermute | solution.py:315
  74.1 9.0 %collective-permute-start.112 = (f32[5,8,128]{2,1,0:T(8,128)S(1)}, f32[5,8,128]{2,1,0:T(8,128)S(1)}, u32[]{:S(2)}, u32[]{:S(2)}) collective-permute-start(f32[5,8,128]{2,1,0:T(8,128)S(1)} %param.112), channel_id=1, source_target_pairs={{512,1},{544,33},{576,65},{608,97},{640,129},{672,161},{704,193},{... | collective-permute-start | bytes 61448 | tf_op jit(solution)/shard_map/cond/branch_16_fun/ppermute | solution.py:302

commit v3 on v2

--- a/solution.py
+++ b/solution.py
@@ -41,7 +41,15 @@
     return lax.axis_index(axis) % 2 == 0
 
 
-def radial_out(state, eddy, inner, outer):
+def radial_out(state_in, eddy_in, inner, outer, state, eddy, done):
+    copies = [
+        pltpu.make_async_copy(state_in, state, done.at[0]),
+        pltpu.make_async_copy(eddy_in, eddy, done.at[1]),
+    ]
+    for copy in copies:
+        copy.start()
+    for copy in copies:
+        copy.wait()
     upper = subs() < 4
     even_rad = is_even("rad")
     for field in range(NV + 1):
@@ -70,7 +78,7 @@
 
 
 def edges_kernel(section):
-    def kernel(field, eddy, received, matrix, face, inner, outer):
+    def kernel(field, eddy, received, matrix, face, outer, inner):
         lane = lanes()
         even = is_even("circ")
         ghost = interpolated(received, matrix, section)
@@ -93,8 +101,8 @@
             for var in range(NV):
                 for a in (0, CA - 1):
                     k = 88 + var * CA + a
-                    first = place(first, ghost[var, rows], 0, k)
-                    last = place(last, ghost[var, rows], 127, k)
+                    first = place(first, ghost_tile(ghost, section, var, half), 0, k)
+                    last = place(last, ghost_tile(ghost, section, var, half), 127, k)
             inner[rows] = jnp.where(even, last, first)
             outer[rows] = jnp.where(even, first, last)
 
@@ -111,10 +119,39 @@
 
 
 def interpolated(received, matrix, section):
-    rows = received.shape[1]
-    flat = received[...].reshape(NV * rows, 128)
+    count = received.shape[0]
+    flat = received[...].reshape(count * 8, 128)
     ghost = jnp.dot(flat, matrix[section], precision=lax.Precision.HIGHEST, preferred_element_type=F32)
-    return ghost.reshape(NV, rows, 128)
+    return ghost.reshape(count, 8, 128)
+
+
+SHARED = (1, 2, 4)
+
+
+def plane_tiles(section):
+    return NV if section == 3 else NV + -(-NV // SHARED[section])
+
+
+def write_plane(plane, section, own, halo):
+    for v in range(NV):
+        plane[v] = own[v]
+    if section == 3:
+        return
+    shared = SHARED[section]
+    shift, need, sub = 8 // shared, 3 - section, subs()
+    for start in range(0, NV, shared):
+        tile = halo[start]
+        for v in range(start + 1, min(start + shared, NV)):
+            row = (sub + 8 - shift * (v - start)) % 8
+            tile = jnp.where((row < need) | (row >= 8 - need), turn(halo[v], shift * (v - start), 0), tile)
+        plane[NV + start // shared] = tile
+
+
+def ghost_tile(ghost, section, v, half):
+    if half == 0:
+        return ghost[v]
+    shared = SHARED[section]
+    return turn(ghost[NV + v // shared], -(8 // shared) * (v % shared), 0)
 
 
 def side_column(tile, other, own, west, is_rotor, swirl):
@@ -141,7 +178,7 @@
     return e * lap - (0.5 * swirl) * dc - (0.5 * AXIAL_MACH) * da - 0.5 * flux
 
 
-def assemble(state, eddy, from_inner, from_outer, ext, eddy_ext, plane):
+def assemble(state, eddy, from_outer, from_inner, ext, eddy_ext, plane):
     upper = subs() < 4
     is_rotor = lax.axis_index("ax") == 1
     even_rad = is_even("rad")
@@ -168,9 +205,8 @@
             far_row.append(far)
         tiles[0].append(own_row)
         tiles[1].append(far_row)
-    for half in range(2):
-        for var in range(NV):
-            plane[var, pl.ds(8 * half, 8)] = jnp.where(is_rotor, tiles[half][var][0], tiles[half][var][CA - 1])
+    planes = [[jnp.where(is_rotor, row[0], row[CA - 1]) for row in tiles[half]] for half in range(2)]
+    write_plane(plane, 0, *planes)
 
 
 def section_kernel(section):
@@ -183,9 +219,9 @@
         acc_in = None if first else refs.pop(0)
         eddy = refs.pop(0)
         if paired:
-            face, own_inner, own_outer, from_inner, from_outer = refs[:5]
+            face, own_outer, own_inner, from_outer, from_inner = refs[:5]
             refs = refs[5:]
-            start_inner, start_outer = (from_inner, from_outer) if first else (refs.pop(0), refs.pop(0))
+            start_outer, start_inner = (from_outer, from_inner) if first else (refs.pop(0), refs.pop(0))
             ghost = face[...]
         else:
             received, matrix, sides_in = refs[:3]
@@ -245,7 +281,7 @@
                     cn = jnp.where(lane == 127, turn(east, 127 - k), turn(c, -1))
                     up = turn(jnp.where(sub == 0, o, c), 7, 0)
                     dn = turn(jnp.where(sub == 7, o, c), 1, 0)
-                    g = ghost[v, rows]
+                    g = ghost_tile(ghost, section, v, half)
                     lo = tile(v, a - 1, half) if a > 0 else jnp.where(is_rotor, g, zero)
                     hi = tile(v, a + 1, half) if a < CA - 1 else jnp.where(is_rotor, zero, g)
                     dc.append(cn - cp)
@@ -265,9 +301,12 @@
                     nxt[v, a, rows] = u
                     if half == 0:
                         acc_out[v, a] = (base[v, a, 0:8] if first else acc_in[v, a]) + gain * slope
-            if half < send_halves:
-                for v in range(NV):
-                    plane[v, rows] = jnp.where(is_rotor, nxt[v, 0, rows], nxt[v, CA - 1, rows])
+        if not last:
+            planes = [
+                [jnp.where(is_rotor, nxt[v, 0, 8 * h : 8 * h + 8], nxt[v, CA - 1, 8 * h : 8 * h + 8]) for v in range(NV)]
+                for h in range(2)
+            ]
+            write_plane(plane, section + 1, *planes)
 
     return kernel
 
@@ -276,7 +315,7 @@
     if section == 3:
         return call(section_kernel(3), jax.ShapeDtypeStruct((NV, CA, 8, 128), F32), *args)
     rows = 8 if section == 2 else 16
-    shapes = (sds(NV, CA, 16, 128), sds(NV, CA, 8, 128), sds(NV, rows, 128))
+    shapes = (sds(NV, CA, 16, 128), sds(NV, CA, 8, 128), sds(plane_tiles(section + 1), 8, 128))
     if section != 1:
         shapes += (sds(2, rows, 128),)
     return call(section_kernel(section), shapes, *args)
@@ -310,11 +349,11 @@
 
 def beside(section, field, eddy, received, matrix):
     count = lax.axis_size("circ")
-    shapes = (sds(NV, 16, 128), sds(16, 128), sds(16, 128))
-    face, inner, outer = call(edges_kernel(section), shapes, field, eddy, received, matrix)
+    shapes = (sds(plane_tiles(section), 8, 128), sds(16, 128), sds(16, 128))
+    face, outer, inner = call(edges_kernel(section), shapes, field, eddy, received, matrix)
     from_outer = lax.ppermute(outer, "circ", outer_pairs(count, True))
     from_inner = lax.ppermute(inner, "circ", inner_pairs(count))
-    return face, inner, outer, from_inner, from_outer
+    return face, outer, inner, from_outer, from_inner
 
 
 def local(state, eddy, offsets, stencil_index, stencil_weight):
@@ -322,16 +361,24 @@
     weight = jnp.transpose(stencil_weight, (0, 1, 3, 2))
     count = lax.axis_size("rad")
     message = sds(NV + 1, CA // 2, 8, 128)
-    inner, outer = call(radial_out, (message, message), state, eddy)
+    vmem = pl.BlockSpec(memory_space=pltpu.VMEM)
+    inner, outer, own_state, own_eddy = pl.pallas_call(
+        radial_out,
+        in_specs=[pl.BlockSpec(memory_space=pl.ANY)] * 2,
+        out_specs=(vmem,) * 4,
+        out_shape=(message, message, sds(*state.shape), sds(*eddy.shape)),
+        scratch_shapes=[pltpu.SemaphoreType.DMA((2,))],
+        interpret=INTERPRET,
+    )(state, eddy)
     from_outer = lax.ppermute(outer, "rad", outer_pairs(count, False))
     from_inner = lax.ppermute(inner, "rad", inner_pairs(count))
     matrix = call(matrices, sds(4, 128, 128), index, weight)
     places = [offsets[section] for section in range(4)]
-    from_inner, from_outer, matrix, *places = lax.optimization_barrier((from_inner, from_outer, matrix, *places))
+    from_outer, from_inner, matrix, *places = lax.optimization_barrier((from_outer, from_inner, matrix, *places))
     ext, eddy_ext, plane = call(
         assemble,
-        (sds(NV, CA, 16, 128), sds(CA, 16, 128), sds(NV, 16, 128)),
-        state, eddy, from_inner, from_outer,
+        (sds(NV, CA, 16, 128), sds(CA, 16, 128), sds(plane_tiles(0), 8, 128)),
+        own_state, own_eddy, from_outer, from_inner,
     )
     received = ghost_of(places[0], plane)
     edges = beside(0, ext, eddy_ext, received, matrix)

time: 85.5 us -> 83.1 us (0.972)
  starting transfers between devices: 53.8 us -> 49.1 us
  waiting for transfers between devices: 20.6 us -> 23.9 us
  local copies, waits for them, and re-layouts: 2.84 us -> 1.14 us
  Pallas kernels: 3.79 us -> 4.76 us
    ppermute x2, starting transfers between devices: 7.11 us -> 3.84 us  [beside(): from_inner = lax.ppermute(inner, 'circ', inner_pairs(count))]
    ppermute x1, waiting for transfers between devices: 0.01 us -> 2.68 us  [local(): from_inner = lax.ppermute(inner, 'rad', inner_pairs(count))]
    ppermute x2, waiting for transfers between devices: 0.01 us -> 2.42 us  [beside(): from_inner = lax.ppermute(inner, 'circ', inner_pairs(count))]
    ppermute x4, waiting for transfers between devices: 16.1 us -> 13.9 us  [facing(): ghost = lax.ppermute(plane, ('circ', 'ax'), pairs)]
    unnamed x12 -> x6, local copies, waits for them, and re-layouts: 2.17 us -> 0.49 us
    ppermute x2, waiting for transfers between devices: 3.04 us -> 4.34 us  [beside(): from_outer = lax.ppermute(outer, 'circ', outer_pairs(count, True))]
    pallas_call x0 -> x1, Pallas kernels: none -> 0.98 us  [local(): pl.pallas_call(radial_out, in_specs=[pl.BlockSpec(memory_space=pl.ANY)] *...]
    ppermute x1, starting transfers between devices: 5.74 us -> 4.78 us  [local(): from_outer = lax.ppermute(outer, 'rad', outer_pairs(count, False))]
  transfers between devices with their start and end apart: 10 -> 10, of which waited for: 7 -> 8; matrix products, arithmetic and copies ran while one was open for 1% -> 1% of each run, Pallas kernels for 0% -> 0%
where the time goes in v3:
time: 83.1 us; the launch traced here: 81.7 us
  starting transfers between devices  49.1 us (59%)
  waiting for transfers between devices  23.9 us (29%)
  Pallas kernels  4.76 us (6%)
  between operations  2.59 us (3%)
  local copies, waits for them, and re-layouts  1.14 us (1%)
    ppermute x2, starting transfers between devices, beside(): from_outer = lax.ppermute(outer, 'circ', outer_pairs(count, True))  27.6 us
    ppermute x4, waiting for transfers between devices, facing(): ghost = lax.ppermute(plane, ('circ', 'ax'), pairs)  13.9 us
    ppermute x4, starting transfers between devices, facing(): ghost = lax.ppermute(plane, ('circ', 'ax'), pairs)  10.9 us
    ppermute x1, starting transfers between devices, local(): from_outer = lax.ppermute(outer, 'rad', outer_pairs(count, False))  4.78 us
    ppermute x2, waiting for transfers between devices, beside(): from_outer = lax.ppermute(outer, 'circ', outer_pairs(count, True))  4.34 us
    ppermute x2, starting transfers between devices, beside(): from_inner = lax.ppermute(inner, 'circ', inner_pairs(count))  3.84 us
    pallas_call x12, Pallas kernels, call(): pl.pallas_call(kernel, in_specs=[spec] * len(args), out_specs=(spec,) * l...  3.78 us
    ppermute x1, waiting for transfers between devices, local(): from_inner = lax.ppermute(inner, 'rad', inner_pairs(count))  2.68 us
  transfers between devices with their start and end apart: 10, of which 8 were waited for; matrix products, arithmetic and copies ran while one was open for 1% of the time, Pallas kernels for 0%

profile of v3, /device:TPU:50, one launch (start us, length us, event | category | flops | bytes accessed | tf_op | source)
XLA Modules:
  0.0 81.7 jit_solution(15708762212764829286)
XLA Ops:
  0.0 0.0 copy-start
  0.0 0.0 copy-start.1
  0.0 1.0 %shard_map.55 = (f32[6,4,8,128]{3,2,1,0:T(8,128)S(1)}, f32[6,4,8,128]{3,2,1,0:T(8,128)S(1)}, f32[5,8,8,128]{3,2,1,0:T(8,128)S(1)}, f32[8,8,128]{2,1,0:T(8,128)S(1)}) custom-call(f32[5,8,8,128]{3,2,1,0:T(8,128)} %state_in.1, f32[8,8,128]{2,1,0:T(8,128)} %eddy_in.1), custom_call_target="tpu_custom_call" | custom-call | tf_op jit(solution)/shard_map/pallas_call | solution.py:365
  1.0 4.8 %collective-permute-start.128 = (f32[6,4,8,128]{3,2,1,0:T(8,128)S(1)}, f32[6,4,8,128]{3,2,1,0:T(8,128)S(1)}, u32[]{:S(2)}, u32[]{:S(2)}) collective-permute-start(f32[6,4,8,128]{3,2,1,0:T(8,128)S(1)} %get-tuple-element.298), channel_id=1, source_target_pairs={{2,4},{4,2},{6,8},{8,6},{10,12},{12,10},{14,16},{16,14},{18,20},{2... | collective-permute-start | bytes 294920 | tf_op jit(solution)/shard_map/ppermute | solution.py:373
  5.8 1.9 %collective-permute-start.129 = (f32[6,4,8,128]{3,2,1,0:T(8,128)S(1)}, f32[6,4,8,128]{3,2,1,0:T(8,128)S(1)}, u32[]{:S(2)}, u32[]{:S(2)}) collective-permute-start(f32[6,4,8,128]{3,2,1,0:T(8,128)S(1)} %get-tuple-element.299), channel_id=1, source_target_pairs={{0,2},{2,0},{4,6},{6,4},{8,10},{10,8},{12,14},{14,12},{16,18},{18,... | collective-permute-start | bytes 294920 | tf_op jit(solution)/shard_map/ppermute | solution.py:374
  7.7 0.0 copy-done
  7.7 0.0 copy-done.1
  7.7 0.0 copy-start.2
  7.7 0.2 shard_map.56.matrix.refs_5_
  7.9 0.5 copy-done.2
  8.4 0.7 fusion
  9.0 0.6 collective-permute-done.128.from_outer
  9.6 2.7 %collective-permute-done.129.from_inner = f32[6,4,8,128]{3,2,1,0:T(8,128)S(1)} collective-permute-done((f32[6,4,8,128]{3,2,1,0:T(8,128)S(1)}, f32[6,4,8,128]{3,2,1,0:T(8,128)S(1)}, u32[]{:S(2)}, u32[]{:S(2)}) %collective-permute-start.129) | collective-permute-done | bytes 98336 | tf_op jit(solution)/shard_map/ppermute | solution.py:374
  13.0 5.4 %conditional.4 = (f32[10,8,128]{2,1,0:T(8,128)S(1)}) conditional(s32[]{:T(128)} %clamp.12, f32[10,8,128]{2,1,0:T(8,128)S(1)} %get-tuple-element.305, f32[10,8,128]{2,1,0:T(8,128)S(1)} %get-tuple-element.305, f32[10,8,128]{2,1,0:T(8,128)S(1)} %get-tuple-element.305, f32[10,8,128]{2,1,0:T(8,128)S(1)} %get-tuple-element.305, ...), branch_computations={%region_0.0_spmd, %region_1.0_spmd, %region_2.0_spmd, %region_3.0_... | conditional | bytes 163888 | solution.py:347
  13.0 3.2 %collective-permute-start.31 = (f32[10,8,128]{2,1,0:T(8,128)S(1)}, f32[10,8,128]{2,1,0:T(8,128)S(1)}, u32[]{:S(2)}, u32[]{:S(2)}) collective-permute-start(f32[10,8,128]{2,1,0:T(8,128)S(1)} %param.31), channel_id=1, source_target_pairs={{992,1},{0,33},{32,65},{64,97},{96,129},{128,161},{160,193},{192,2... | collective-permute-start | bytes 122888 | tf_op jit(solution)/shard_map/cond/branch_31_fun/ppermute | solution.py:341
  16.3 2.1 %collective-permute-done.31.source = f32[10,8,128]{2,1,0:T(8,128)S(1)} collective-permute-done((f32[10,8,128]{2,1,0:T(8,128)S(1)}, f32[10,8,128]{2,1,0:T(8,128)S(1)}, u32[]{:S(2)}, u32[]{:S(2)}) %collective-permute-start.31) | collective-permute-done | bytes 40992 | tf_op jit(solution)/shard_map/cond/branch_31_fun/ppermute | solution.py:341
  18.4 0.5 shard_map.58
  18.9 24.7 %collective-permute-start.130 = (f32[16,128]{1,0:T(8,128)S(1)}, f32[16,128]{1,0:T(8,128)S(1)}, u32[]{:S(2)}, u32[]{:S(2)}) collective-permute-start(f32[16,128]{1,0:T(8,128)S(1)} %get-tuple-element.308.refs_3_), channel_id=1, source_target_pairs={{0,992},{32,64},{64,32},{96,128},{128,96},{160,192},{192,160},{224... | collective-permute-start | bytes 24584 | tf_op jit(solution)/shard_map/ppermute | solution.py:354
  43.6 1.9 %collective-permute-start.131 = (f32[16,128]{1,0:T(8,128)S(1)}, f32[16,128]{1,0:T(8,128)S(1)}, u32[]{:S(2)}, u32[]{:S(2)}) collective-permute-start(f32[16,128]{1,0:T(8,128)S(1)} %get-tuple-element.309.refs_4_), channel_id=1, source_target_pairs={{0,32},{32,0},{64,96},{96,64},{128,160},{160,128},{192,224},{224,1... | collective-permute-start | bytes 24584 | tf_op jit(solution)/shard_map/ppermute | solution.py:355
  46.7 0.0 collective-permute-done.130.refs_5_.refs_9_
  46.7 2.4 %collective-permute-done.131.refs_6_.refs_10_ = f32[16,128]{1,0:T(8,128)S(1)} collective-permute-done((f32[16,128]{1,0:T(8,128)S(1)}, f32[16,128]{1,0:T(8,128)S(1)}, u32[]{:S(2)}, u32[]{:S(2)}) %collective-permute-start.131) | collective-permute-done | bytes 8224 | tf_op jit(solution)/shard_map/ppermute | solution.py:355
  49.1 0.8 shard_map.59
  49.9 3.1 %conditional.5 = (f32[8,8,128]{2,1,0:T(8,128)S(1)}) conditional(s32[]{:T(128)} %clamp.13, f32[8,8,128]{2,1,0:T(8,128)S(1)} %get-tuple-element.313, f32[8,8,128]{2,1,0:T(8,128)S(1)} %get-tuple-element.313, f32[8,8,128]{2,1,0:T(8,128)S(1)} %get-tuple-element.313, f32[8,8,128]{2,1,0:T(8,128)S(1)} %get-tuple-element.313, ...), branch_computations={%region_32.0_spmd, %region_33.0_spmd, %region_34.0_spmd, %region_3... | conditional | bytes 131120 | solution.py:347
  49.9 1.9 %collective-permute-start.32 = (f32[8,8,128]{2,1,0:T(8,128)S(1)}, f32[8,8,128]{2,1,0:T(8,128)S(1)}, u32[]{:S(2)}, u32[]{:S(2)}) collective-permute-start(f32[8,8,128]{2,1,0:T(8,128)S(1)} %param.32), channel_id=1, source_target_pairs={{0,1},{32,33},{64,65},{96,97},{128,129},{160,161},{192,193},{224,2... | collective-permute-start | bytes 98312 | tf_op jit(solution)/shard_map/cond/branch_0_fun/ppermute | solution.py:341
  51.8 1.2 %collective-permute-done.32.source = f32[8,8,128]{2,1,0:T(8,128)S(1)} collective-permute-done((f32[8,8,128]{2,1,0:T(8,128)S(1)}, f32[8,8,128]{2,1,0:T(8,128)S(1)}, u32[]{:S(2)}, u32[]{:S(2)}) %collective-permute-start.32) | collective-permute-done | bytes 32800 | tf_op jit(solution)/shard_map/cond/branch_0_fun/ppermute | solution.py:341
  53.0 0.4 shard_map.60
  53.5 7.5 %conditional.6 = (f32[7,8,128]{2,1,0:T(8,128)S(1)}) conditional(s32[]{:T(128)} %clamp.14, f32[7,8,128]{2,1,0:T(8,128)S(1)} %get-tuple-element.318, f32[7,8,128]{2,1,0:T(8,128)S(1)} %get-tuple-element.318, f32[7,8,128]{2,1,0:T(8,128)S(1)} %get-tuple-element.318, f32[7,8,128]{2,1,0:T(8,128)S(1)} %get-tuple-element.318, ...), branch_computations={%region_64.0_spmd, %region_65.0_spmd, %region_66.0_spmd, %region_6... | conditional | bytes 114736 | solution.py:347
  53.5 3.2 %collective-permute-start.72 = (f32[7,8,128]{2,1,0:T(8,128)S(1)}, f32[7,8,128]{2,1,0:T(8,128)S(1)}, u32[]{:S(2)}, u32[]{:S(2)}) collective-permute-start(f32[7,8,128]{2,1,0:T(8,128)S(1)} %param.72), channel_id=1, source_target_pairs={{256,1},{288,33},{320,65},{352,97},{384,129},{416,161},{448,193},{... | collective-permute-start | bytes 86024 | tf_op jit(solution)/shard_map/cond/branch_8_fun/ppermute | solution.py:341
  56.7 4.2 %collective-permute-done.72.source = f32[7,8,128]{2,1,0:T(8,128)S(1)} collective-permute-done((f32[7,8,128]{2,1,0:T(8,128)S(1)}, f32[7,8,128]{2,1,0:T(8,128)S(1)}, u32[]{:S(2)}, u32[]{:S(2)}) %collective-permute-start.72) | collective-permute-done | bytes 28704 | tf_op jit(solution)/shard_map/cond/branch_8_fun/ppermute | solution.py:341
  60.9 0.5 shard_map.61
  61.4 2.9 %collective-permute-start.132 = (f32[16,128]{1,0:T(8,128)S(1)}, f32[16,128]{1,0:T(8,128)S(1)}, u32[]{:S(2)}, u32[]{:S(2)}) collective-permute-start(f32[16,128]{1,0:T(8,128)S(1)} %get-tuple-element.320.refs_5_), channel_id=1, source_target_pairs={{0,992},{32,64},{64,32},{96,128},{128,96},{160,192},{192,160},{224... | collective-permute-start | bytes 24584 | tf_op jit(solution)/shard_map/ppermute | solution.py:354
  64.3 1.9 %collective-permute-start.133 = (f32[16,128]{1,0:T(8,128)S(1)}, f32[16,128]{1,0:T(8,128)S(1)}, u32[]{:S(2)}, u32[]{:S(2)}) collective-permute-start(f32[16,128]{1,0:T(8,128)S(1)} %get-tuple-element.321.refs_6_), channel_id=1, source_target_pairs={{0,32},{32,0},{64,96},{96,64},{128,160},{160,128},{192,224},{224,1... | collective-permute-start | bytes 24584 | tf_op jit(solution)/shard_map/ppermute | solution.py:355
  66.9 4.3 %collective-permute-done.132.refs_7_ = f32[16,128]{1,0:T(8,128)S(1)} collective-permute-done((f32[16,128]{1,0:T(8,128)S(1)}, f32[16,128]{1,0:T(8,128)S(1)}, u32[]{:S(2)}, u32[]{:S(2)}) %collective-permute-start.132) | collective-permute-done | bytes 8224 | tf_op jit(solution)/shard_map/ppermute | solution.py:354
  71.2 0.0 collective-permute-done.133.refs_8_
  71.2 0.5 shard_map.62
  71.7 9.1 %conditional.7 = (f32[5,8,128]{2,1,0:T(8,128)S(1)}) conditional(s32[]{:T(128)} %clamp.15, f32[5,8,128]{2,1,0:T(8,128)S(1)} %get-tuple-element.325, f32[5,8,128]{2,1,0:T(8,128)S(1)} %get-tuple-element.325, f32[5,8,128]{2,1,0:T(8,128)S(1)} %get-tuple-element.325, f32[5,8,128]{2,1,0:T(8,128)S(1)} %get-tuple-element.325, ...), branch_computations={%region_96.0_spmd, %region_97.0_spmd, %region_98.0_spmd, %region_9... | conditional | bytes 81968 | solution.py:347
  71.7 2.6 %collective-permute-start.112 = (f32[5,8,128]{2,1,0:T(8,128)S(1)}, f32[5,8,128]{2,1,0:T(8,128)S(1)}, u32[]{:S(2)}, u32[]{:S(2)}) collective-permute-start(f32[5,8,128]{2,1,0:T(8,128)S(1)} %param.112), channel_id=1, source_target_pairs={{512,1},{544,33},{576,65},{608,97},{640,129},{672,161},{704,193},{... | collective-permute-start | bytes 61448 | tf_op jit(solution)/shard_map/cond/branch_16_fun/ppermute | solution.py:341
  74.4 6.4 %collective-permute-done.112.source = f32[5,8,128]{2,1,0:T(8,128)S(1)} collective-permute-done((f32[5,8,128]{2,1,0:T(8,128)S(1)}, f32[5,8,128]{2,1,0:T(8,128)S(1)}, u32[]{:S(2)}, u32[]{:S(2)}) %collective-permute-start.112) | collective-permute-done | bytes 20512 | tf_op jit(solution)/shard_map/cond/branch_16_fun/ppermute | solution.py:341
  80.8 0.9 %shard_map.63 = f32[5,8,8,128]{3,2,1,0:T(8,128)} custom-call(f32[5,8,16,128]{3,2,1,0:T(8,128)S(1)} %get-tuple-element.322.refs_0_, f32[5,8,16,128]{3,2,1,0:T(8,128)S(1)} %get-tuple-element.302.field.refs_0_.refs_1_, f32[5,8,8,128]{3,2,1,0:T(8,128)S(1)} %get-tuple-element.323.refs_2_, f32[8,16,128]{2,1,0:T(8,128)S(1)} %get-tuple-element.303.eddy.refs_1_.refs_3_, ...), custom_call_target="tpu_custom_call" | custom-call | tf_op jit(solution)/shard_map/pallas_call | solution.py:19
  (5 shorter events, 0.1 us)
Async XLA Ops:
  0.0 7.7 %copy-start = (s32[2,4,128,4]{2,3,1,0:T(4,128)S(1)}, s32[2,4,128,4]{2,3,1,0:T(4,128)}, u32[]{:S(2)}) copy-start(s32[2,4,128,4]{2,3,1,0:T(4,128)} %param.136) | copy-start | bytes 49156
  0.0 7.7 %copy-start.1 = (f32[2,4,128,4]{2,3,1,0:T(4,128)S(1)}, f32[2,4,128,4]{2,3,1,0:T(4,128)}, u32[]{:S(2)}) copy-start(f32[2,4,128,4]{2,3,1,0:T(4,128)} %param.137) | copy-start | bytes 49156
  1.0 8.6 %collective-permute-start.128 = (f32[6,4,8,128]{3,2,1,0:T(8,128)S(1)}, f32[6,4,8,128]{3,2,1,0:T(8,128)S(1)}, u32[]{:S(2)}, u32[]{:S(2)}) collective-permute-start(f32[6,4,8,128]{3,2,1,0:T(8,128)S(1)} %get-tuple-element.298), channel_id=1, source_target_pairs={{2,4},{4,2},{6,8},{8,6},{10,12},{12,10},{14,16},{16,14},{18,20},{2... | collective-permute-start | bytes 294920 | tf_op jit(solution)/shard_map/ppermute | solution.py:373
  5.8 6.5 %collective-permute-start.129 = (f32[6,4,8,128]{3,2,1,0:T(8,128)S(1)}, f32[6,4,8,128]{3,2,1,0:T(8,128)S(1)}, u32[]{:S(2)}, u32[]{:S(2)}) collective-permute-start(f32[6,4,8,128]{3,2,1,0:T(8,128)S(1)} %get-tuple-element.299), channel_id=1, source_target_pairs={{0,2},{2,0},{4,6},{6,4},{8,10},{10,8},{12,14},{14,12},{16,18},{18,... | collective-permute-start | bytes 294920 | tf_op jit(solution)/shard_map/ppermute | solution.py:374
  7.7 0.7 copy-start.2
  13.0 5.3 %collective-permute-start.31 = (f32[10,8,128]{2,1,0:T(8,128)S(1)}, f32[10,8,128]{2,1,0:T(8,128)S(1)}, u32[]{:S(2)}, u32[]{:S(2)}) collective-permute-start(f32[10,8,128]{2,1,0:T(8,128)S(1)} %param.31), channel_id=1, source_target_pairs={{992,1},{0,33},{32,65},{64,97},{96,129},{128,161},{160,193},{192,2... | collective-permute-start | bytes 122888 | tf_op jit(solution)/shard_map/cond/branch_31_fun/ppermute | solution.py:341
  18.9 27.8 %collective-permute-start.130 = (f32[16,128]{1,0:T(8,128)S(1)}, f32[16,128]{1,0:T(8,128)S(1)}, u32[]{:S(2)}, u32[]{:S(2)}) collective-permute-start(f32[16,128]{1,0:T(8,128)S(1)} %get-tuple-element.308.refs_3_), channel_id=1, source_target_pairs={{0,992},{32,64},{64,32},{96,128},{128,96},{160,192},{192,160},{224... | collective-permute-start | bytes 24584 | tf_op jit(solution)/shard_map/ppermute | solution.py:354
  43.6 5.5 %collective-permute-start.131 = (f32[16,128]{1,0:T(8,128)S(1)}, f32[16,128]{1,0:T(8,128)S(1)}, u32[]{:S(2)}, u32[]{:S(2)}) collective-permute-start(f32[16,128]{1,0:T(8,128)S(1)} %get-tuple-element.309.refs_4_), channel_id=1, source_target_pairs={{0,32},{32,0},{64,96},{96,64},{128,160},{160,128},{192,224},{224,1... | collective-permute-start | bytes 24584 | tf_op jit(solution)/shard_map/ppermute | solution.py:355
  49.9 3.1 %collective-permute-start.32 = (f32[8,8,128]{2,1,0:T(8,128)S(1)}, f32[8,8,128]{2,1,0:T(8,128)S(1)}, u32[]{:S(2)}, u32[]{:S(2)}) collective-permute-start(f32[8,8,128]{2,1,0:T(8,128)S(1)} %param.32), channel_id=1, source_target_pairs={{0,1},{32,33},{64,65},{96,97},{128,129},{160,161},{192,193},{224,2... | collective-permute-start | bytes 98312 | tf_op jit(solution)/shard_map/cond/branch_0_fun/ppermute | solution.py:341
  53.5 7.4 %collective-permute-start.72 = (f32[7,8,128]{2,1,0:T(8,128)S(1)}, f32[7,8,128]{2,1,0:T(8,128)S(1)}, u32[]{:S(2)}, u32[]{:S(2)}) collective-permute-start(f32[7,8,128]{2,1,0:T(8,128)S(1)} %param.72), channel_id=1, source_target_pairs={{256,1},{288,33},{320,65},{352,97},{384,129},{416,161},{448,193},{... | collective-permute-start | bytes 86024 | tf_op jit(solution)/shard_map/cond/branch_8_fun/ppermute | solution.py:341
  61.4 9.8 %collective-permute-start.132 = (f32[16,128]{1,0:T(8,128)S(1)}, f32[16,128]{1,0:T(8,128)S(1)}, u32[]{:S(2)}, u32[]{:S(2)}) collective-permute-start(f32[16,128]{1,0:T(8,128)S(1)} %get-tuple-element.320.refs_5_), channel_id=1, source_target_pairs={{0,992},{32,64},{64,32},{96,128},{128,96},{160,192},{192,160},{224... | collective-permute-start | bytes 24584 | tf_op jit(solution)/shard_map/ppermute | solution.py:354
  64.3 6.9 %collective-permute-start.133 = (f32[16,128]{1,0:T(8,128)S(1)}, f32[16,128]{1,0:T(8,128)S(1)}, u32[]{:S(2)}, u32[]{:S(2)}) collective-permute-start(f32[16,128]{1,0:T(8,128)S(1)} %get-tuple-element.321.refs_6_), channel_id=1, source_target_pairs={{0,32},{32,0},{64,96},{96,64},{128,160},{160,128},{192,224},{224,1... | collective-permute-start | bytes 24584 | tf_op jit(solution)/shard_map/ppermute | solution.py:355
  71.7 9.0 %collective-permute-start.112 = (f32[5,8,128]{2,1,0:T(8,128)S(1)}, f32[5,8,128]{2,1,0:T(8,128)S(1)}, u32[]{:S(2)}, u32[]{:S(2)}) collective-permute-start(f32[5,8,128]{2,1,0:T(8,128)S(1)} %param.112), channel_id=1, source_target_pairs={{512,1},{544,33},{576,65},{608,97},{640,129},{672,161},{704,193},{... | collective-permute-start | bytes 61448 | tf_op jit(solution)/shard_map/cond/branch_16_fun/ppermute | solution.py:341
